TPU v7x, 128 devices: a whole 4x4x4 slice. The times are simulated.
128 devices in a mesh: dp: 32 (over y, x, core), tp: 4 (over z).
Axes of the slice: x: 4, y: 4, z: 4, core: 2. Of those that a mesh axis runs over, the one named last changes fastest.
Arguments:
- tokens: bfloat16 [16384, 4096], P(('dp', 'tp')), may hold values from -6 to 6
- norm_gain: float32 [4096], replicated, may hold values from 0.1 to 1.9
- w_query: bfloat16 [4096, 4096], P(None, 'tp'), may hold values from -0.09375 to 0.09375
- w_key: bfloat16 [4096, 1024], P(None, 'tp'), may hold values from -2.34375 to 2.34375
- w_value: bfloat16 [4096, 1024], P(None, 'tp'), may hold values from -0.09375 to 0.09375
- w_output: bfloat16 [4096, 4096], P('tp'), may hold values from -0.09375 to 0.09375
- doc_lengths: int32 [128], replicated, may hold values from 1 to 512, as said below
- pack_index: int32 [16384], replicated, may hold values from 0 to 16383, as said below
Outputs:
- output: bfloat16 [16384, 4096], P(('dp', 'tp'))
Inputs may be any that keep to these rules, and one draw needn't show every extreme that they name: `doc_lengths`: each run of 4 documents numbered g * 4 to g * 4 + 4 - 1 (the documents of group g) holds at most 1024 tokens together, and some group holds exactly 1024. No document is longer than 512 tokens, and one has exactly that many. `pack_index`: each packed position appears once. The 128 rows of one device hold at most 8 tokens of the documents of any one group; every device holds the same number of one group's tokens, up to one.
All inputs are finite; a program needn't handle non-finite values.
Results may differ from a plain program's by a relative error of at most 0.01.
Values may be sent and summed in bfloat16 or wider, within the bound.
No kernel may reach another device: no remote copies, remote signals or barrier semaphores. Data moves between devices by JAX's collectives and lax.ppermute only.
A program may use at most 128 MiB of HBM per device.

v0:
```python
import jax
import jax.numpy as jnp
from jax import lax
from jax.sharding import PartitionSpec as P

HEAD_DIM = 128
GROUP_DOCS = 4


rope_base = 500000.0
norm_eps = 1e-05
score_floor = -1e30


def split_up(array, dim, length):
    dims = array.shape
    pieces = array.reshape(*dims[:dim], length, dims[dim] // length, *dims[dim + 1 :])
    return jnp.moveaxis(pieces, dim, 0)


def sum_at_owner(array, axis, dim):
    pieces = split_up(array, dim, lax.axis_size(axis))
    arrived = lax.all_to_all(pieces, axis, split_axis=0, concat_axis=0, tiled=True)
    return arrived.astype(jnp.float32).sum(axis=0)


def row_tables(pack_index, doc_lengths, group_count, tok_dev):
    doc_ends = jnp.cumsum(doc_lengths)
    doc_starts = doc_ends - doc_lengths
    inside = (
        (pack_index[:, None] >= doc_starts[None, :]) & (pack_index[:, None] < doc_ends[None, :])
    ).astype(jnp.int32)
    doc_index = jnp.sum(inside * jnp.arange(doc_lengths.shape[0], dtype=jnp.int32)[None, :], axis=1)
    position = pack_index - jnp.sum(inside * doc_starts[None, :], axis=1)
    owner_group = doc_index // GROUP_DOCS
    member = (
        owner_group.reshape(-1, tok_dev)[:, :, None]
        == jnp.arange(group_count, dtype=jnp.int32)[None, None, :]
    ).astype(jnp.int32)
    slot_rank = jnp.sum((jnp.cumsum(member, axis=1) - 1) * member, axis=2)
    return (doc_index, position, owner_group, slot_rank.reshape(-1))


def rotate(projected, position, head_count):
    row_count = projected.shape[0]
    half_dim = HEAD_DIM // 2
    spread = projected.reshape(row_count, head_count, HEAD_DIM)
    frequency = rope_base ** (-2.0 * jnp.arange(half_dim, dtype=jnp.float32) / HEAD_DIM)
    angles = position.astype(jnp.float32)[:, None] * frequency[None, :]
    cosine = jnp.cos(angles)[:, None, :]
    sine = jnp.sin(angles)[:, None, :]
    lower_part = spread[:, :, :half_dim]
    upper_part = spread[:, :, half_dim:]
    turned = jnp.concatenate(
        [lower_part * cosine - upper_part * sine, upper_part * cosine + lower_part * sine], axis=2
    )
    return turned.reshape(row_count, head_count * HEAD_DIM)


def attend(query, key_rows, value_rows, segment, places, head_count, kv_count):
    slot_total = query.shape[0]
    group_size = head_count // kv_count
    score_scale = HEAD_DIM ** (-0.5)
    block_rows = min(512, slot_total)
    query_heads = query.reshape(slot_total, kv_count, group_size, HEAD_DIM)
    key_heads = key_rows.reshape(slot_total, kv_count, HEAD_DIM)
    value_heads = value_rows.reshape(slot_total, kv_count, HEAD_DIM)
    outputs = []
    for block_start in range(0, slot_total, block_rows):
        query_block = query_heads[block_start : block_start + block_rows]
        score_values = (
            jnp.einsum("qkgd,skd->kgqs", query_block, key_heads, preferred_element_type=jnp.float32)
            * score_scale
        )
        block_segment = segment[block_start : block_start + block_rows]
        block_places = places[block_start : block_start + block_rows]
        allowed = (block_segment[:, None] == segment[None, :]) & (
            places[None, :] <= block_places[:, None]
        )
        score_values = jnp.where(allowed[None, None], score_values, score_floor)
        row_peak = jnp.max(score_values, axis=-1, keepdims=True)
        weights = jnp.exp(score_values - row_peak)
        weights = (weights / jnp.sum(weights, axis=-1, keepdims=True)).astype(jnp.bfloat16)
        mixed_values = jnp.einsum(
            "kgqs,skd->qkgd", weights, value_heads, preferred_element_type=jnp.float32
        )
        outputs.append(mixed_values.astype(jnp.bfloat16).reshape(block_rows, head_count * HEAD_DIM))
    return jnp.concatenate(outputs, axis=0)


def body(tokens, norm_gain, w_query, w_key, w_value, w_output, doc_lengths, pack_index):
    group_count = lax.axis_size("dp")
    tp_count = lax.axis_size("tp")
    tok_dev = tokens.shape[0]
    model_width = tokens.shape[1]
    send_slots = 2 * tok_dev // group_count
    device_total = group_count * tp_count
    slot_total = device_total * send_slots
    group_rows = group_count * send_slots
    my_group = lax.axis_index("dp")
    my_source = my_group * tp_count + lax.axis_index("tp")
    doc_index, position, owner_group, slot_rank = row_tables(
        pack_index, doc_lengths, group_count, tok_dev
    )
    own_group = lax.dynamic_slice_in_dim(owner_group, my_source * tok_dev, tok_dev)
    own_rank = lax.dynamic_slice_in_dim(slot_rank, my_source * tok_dev, tok_dev)
    send_index = own_group * send_slots + own_rank
    residual = tokens.astype(jnp.float32)
    normed = (
        residual
        * lax.rsqrt(jnp.mean(residual * residual, axis=1, keepdims=True) + norm_eps)
        * norm_gain
    ).astype(jnp.bfloat16)
    outgoing = jnp.zeros((group_rows, model_width), jnp.bfloat16).at[send_index].set(normed)
    fanned = jnp.broadcast_to(
        outgoing.reshape(group_count, 1, send_slots, model_width),
        (group_count, tp_count, send_slots, model_width),
    )
    arrived = lax.all_to_all(
        fanned.reshape(slot_total, model_width),
        ("dp", "tp"),
        split_axis=0,
        concat_axis=0,
        tiled=True,
    )
    mine = (owner_group == my_group).reshape(device_total, tok_dev)
    slot_match = (
        slot_rank.reshape(device_total, tok_dev)[:, :, None]
        == jnp.arange(send_slots, dtype=jnp.int32)[None, None, :]
    )
    pick = (mine[:, :, None] & slot_match).astype(jnp.int32)
    occupied = jnp.sum(pick, axis=1).reshape(slot_total)
    slot_doc = jnp.sum(pick * doc_index.reshape(device_total, tok_dev, 1), axis=1).reshape(
        slot_total
    )
    slot_place = jnp.sum(pick * position.reshape(device_total, tok_dev, 1), axis=1).reshape(
        slot_total
    )
    segment = jnp.where(occupied > 0, slot_doc, -1 - jnp.arange(slot_total, dtype=jnp.int32))
    head_count = w_query.shape[1] // HEAD_DIM
    kv_count = w_key.shape[1] // HEAD_DIM
    query = rotate(
        jnp.dot(arrived, w_query, preferred_element_type=jnp.float32), slot_place, head_count
    ).astype(jnp.bfloat16)
    key_rows = rotate(
        jnp.dot(arrived, w_key, preferred_element_type=jnp.float32), slot_place, kv_count
    ).astype(jnp.bfloat16)
    value_rows = jnp.dot(arrived, w_value, preferred_element_type=jnp.float32).astype(jnp.bfloat16)
    context = attend(query, key_rows, value_rows, segment, slot_place, head_count, kv_count)
    came_back = lax.all_to_all(context, "dp", split_axis=0, concat_axis=0, tiled=True)
    group_span = tp_count * tok_dev
    group_owner = lax.dynamic_slice_in_dim(owner_group, my_group * group_span, group_span)
    group_rank = lax.dynamic_slice_in_dim(slot_rank, my_group * group_span, group_span)
    source_member = jnp.arange(group_span, dtype=jnp.int32) // tok_dev
    fetch_index = group_owner * (tp_count * send_slots) + source_member * send_slots + group_rank
    compact = jnp.take(came_back, fetch_index, axis=0)
    attended = sum_at_owner(
        jnp.dot(compact, w_output, preferred_element_type=jnp.float32).astype(jnp.bfloat16), "tp", 0
    )
    return (residual + attended).astype(jnp.bfloat16)


def solution(mesh):
    placed = (
        P(("dp", "tp"), None),
        P(),
        P(None, "tp"),
        P(None, "tp"),
        P(None, "tp"),
        P("tp", None),
        P(),
        P(),
    )
    return jax.shard_map(
        body, mesh=mesh, in_specs=placed, out_specs=P(("dp", "tp"), None), check_vma=False
    )
```

profile of v0, /device:TPU:0, one launch (start us, length us, event | category | flops | bytes accessed | tf_op | source)
XLA Modules:
  0.0 300.7 jit_solution(13517198028188437393)
XLA Ops:
  1.9 8.0 %select_reduce_fusion = (s32[16384]{0:T(1024)S(1)}, s32[16384]{0:T(1024)S(1)}) fusion(s32[128]{0:T(128)S(1)} %reduce, s32[128]{0:T(128)S(1)} %sub.56, s32[16384]{0:T(1024)} %param.15), kind=kLoop, calls=%fused_computation.23 | loop fusion | flops 14647296 | bytes 197632 | tf_op jit(solution)/shard_map/reduce_sum | solution.py:34
  11.1 1.5 fusion.18
  12.7 4.5 %scatter_custom_fusion = bf16[256,4096]{1,0:T(8,128)(2,1)} fusion(s32[128]{0:T(128)S(1)} %compare_select_fusion.1, bf16[128,4096]{1,0:T(8,128)(2,1)} %param.8, f32[4096]{0:T(1024)} %param.9, f32[128]{0:T(128)S(1)} %add_rsqrt_fusion, bf16[]{:T(256)} %constant.93.clone.1), kind=kCustom, calls=%fused_computation.55 | custom fusion | flops 2097152 | bytes 3162626 | tf_op jit(solution)/shard_map/scatter | solution.py:114
  17.3 5.9 %broadcast_in_dim.39 = bf16[32,4,8,4096]{3,2,1,0:T(8,128)(2,1)} broadcast(bf16[32,8,4096]{2,1,0:T(8,128)(2,1)} %bitcast.96), dimensions={0,2,3} | broadcast | bytes 10485760 | tf_op jit(solution)/shard_map/broadcast_in_dim | solution.py:115
  23.1 11.9 %all-to-all-start = ((bf16[128,8,4096]{2,1,0:T(8,128)(2,1)}), bf16[128,8,4096]{2,1,0:T(8,128)(2,1)}, u32[]{:S(2)}, u32[]{:S(2)}) async-start(bf16[128,8,4096]{2,1,0:T(8,128)(2,1)} %bitcast.95), calls=%async_computation | async-start | bytes 16777216 | tf_op jit(solution)/shard_map/all_to_all | solution.py:119
  35.1 6.5 %select_reduce_fusion.4 = (s32[128,8]{1,0:T(8,128)S(1)}, s32[128,8]{1,0:T(8,128)S(1)}, s32[128,8]{1,0:T(8,128)S(1)}) fusion(s32[128,128]{1,0:T(8,128)S(1)} %bitcast.103, s32[128,128]{1,0:T(8,128)S(1)} %copy.62, pred[128,128]{1,0:T(8,128)(4,1)S(1)} %broadcast_compare_fusion.1, s32[128,128]{1,0:T(8,128)S(1)} %subtract_bitcast_fusion), kind=kLoop, calls=%fused_computation.68 | loop fusion | flops 1045504 | bytes 225280 | tf_op jit(solution)/shard_map/reduce_sum | solution.py:133
  42.2 11.5 %copy.84 = bf16[1024,4096]{1,0:T(8,128)(2,1)} copy(bf16[1024,4096]{0,1:T(8,128)(2,1)} %bitcast.97) | data formatting | bytes 16777216 | tf_op jit(solution)/shard_map/dot_general | solution.py:143
  53.7 4.1 %copy.81 = bf16[256,4096]{1,0:T(8,128)(2,1)} copy(bf16[256,4096]{0,1:T(8,128)(2,1)} %bitcast.101) | data formatting | bytes 4194304 | tf_op jit(solution)/shard_map/dot_general | solution.py:146
  58.8 2.0 compare_and_fusion.2
  60.8 74.4 %all-to-all-done = bf16[128,8,4096]{2,1,0:T(8,128)(2,1)} async-done(((bf16[128,8,4096]{2,1,0:T(8,128)(2,1)}), bf16[128,8,4096]{2,1,0:T(8,128)(2,1)}, u32[]{:S(2)}, u32[]{:S(2)}) %all-to-all-start) | async-done | bytes 8388640 | tf_op jit(solution)/shard_map/all_to_all | solution.py:119
  135.2 12.9 %fusion.4 = f32[1024,8,128]{0,2,1:T(8,128)S(1)} fusion(bf16[8,128,4096]{2,1,0:T(8,128)(2,1)} %bitcast.98, bf16[128,8,4096]{2,1,0:T(8,128)(2,1)} %all-to-all-done), kind=kOutput, calls=%fused_computation.12 | convolution fusion | flops 8589934592 | bytes 20971520 | tf_op jit(solution)/shard_map/dot_general | solution.py:143
  149.7 5.7 %fusion.6 = f32[1024,2,128]{0,2,1:T(8,128)S(1)} fusion(bf16[2,128,4096]{2,1,0:T(8,128)(2,1)S(1)} %bitcast.102, bf16[128,8,4096]{2,1,0:T(8,128)(2,1)} %all-to-all-done), kind=kOutput, calls=%fused_computation.14 | convolution fusion | flops 2147483648 | bytes 11534336 | tf_op jit(solution)/shard_map/dot_general | solution.py:146
  157.5 11.1 %fusion.61 = (f32[2,4,512]{2,1,0:T(4,128)S(1)}, f32[2,4,512,1024]{2,3,1,0:T(8,128)}) fusion(pred[512,1024]{0,1:T(8,128)(4,1)} %get-tuple-element.21, bf16[512,2,4,128]{0,3,2,1:T(8,128)(2,1)} %bitcast.107, bf16[1024,2,64]{0,2,1:T(8,128)(2,1)} %get-tuple-element.17, bf16[1024,2,64]{0,2,1:T(8,128)(2,1)S(1)} %get-tuple-element.16), kind=kOutput, calls=%fused_computation.115 | convolution fusion | flops 1091568640 | bytes 18890752 | tf_op jit(solution)/shard_map/sub | solution.py:82
  168.6 5.9 %fusion.30 = bf16[1024,256]{0,1:T(8,128)(2,1)S(1)} fusion(bf16[4096,256]{1,0:T(8,128)(2,1)S(1)} %copy-done, bf16[128,8,4096]{2,1,0:T(8,128)(2,1)} %all-to-all-done), kind=kOutput, calls=%fused_computation.53 | convolution fusion | flops 2147745792 | bytes 11010048 | tf_op jit(solution)/shard_map/dot_general | solution.py:148
  174.6 2.4 copy-done.7
  177.0 1.5 fusion.28
  179.1 11.2 %fusion.62 = (f32[2,4,512]{2,1,0:T(4,128)S(1)}, f32[2,4,512,1024]{2,3,1,0:T(8,128)}) fusion(pred[512,1024]{0,1:T(8,128)(4,1)} %get-tuple-element.20, bf16[512,2,4,128]{0,3,2,1:T(8,128)(2,1)S(1)} %bitcast.106, bf16[1024,2,64]{0,2,1:T(8,128)(2,1)} %get-tuple-element.17, bf16[1024,2,64]{0,2,1:T(8,128)(2,1)S(1)} %get-tuple-element.16), kind=kOutput, calls=%fused_computation.116 | convolution fusion | flops 1091568640 | bytes 18890752 | tf_op jit(solution)/shard_map/sub | solution.py:82
  190.3 7.1 %fusion.29 = bf16[2,128,4,512]{3,1,2,0:T(8,128)(2,1)S(1)} fusion(bf16[1024,2,128,1]{0,2,3,1:T(8,128)(2,1)S(1)} %bitcast.112, f32[2,4,512,1024]{2,3,1,0:T(8,128)} %get-tuple-element.29, f32[2,4,512]{2,1,0:T(4,128)S(1)} %get-tuple-element.28), kind=kOutput, calls=%fused_computation.52 | convolution fusion | flops 1082654720 | bytes 18366464 | tf_op jit(solution)/shard_map/kgqs,skd->qkgd/dot_general | solution.py:84
  197.9 1.5 pad_maximum_fusion
  199.4 5.7 %all-to-all-start.1 = ((bf16[32,32,1024]{2,1,0:T(8,128)(2,1)}), bf16[32,32,1024]{2,1,0:T(8,128)(2,1)S(1)}, u32[]{:S(2)}, u32[]{:S(2)}) async-start(bf16[32,32,1024]{2,1,0:T(8,128)(2,1)} %bitcast.99), calls=%async_computation.1 | async-start | bytes 4194304 | tf_op jit(solution)/shard_map/all_to_all | solution.py:150
  205.2 30.0 %all-to-all-done.1 = bf16[32,32,1024]{2,1,0:T(8,128)(2,1)S(1)} async-done(((bf16[32,32,1024]{2,1,0:T(8,128)(2,1)}), bf16[32,32,1024]{2,1,0:T(8,128)(2,1)S(1)}, u32[]{:S(2)}, u32[]{:S(2)}) %all-to-all-start.1) | async-done | bytes 2097184 | tf_op jit(solution)/shard_map/all_to_all | solution.py:150
  235.2 2.0 gather_fusion
  237.2 8.3 %convolution_convert_fusion = bf16[512,4096]{1,0:T(8,128)(2,1)S(1)} fusion(bf16[1024,4096]{1,0:T(8,128)(2,1)} %param.13, bf16[512,1024]{1,0:T(8,128)(2,1)S(1)} %gather_fusion, pred[512]{0:T(512)(128)(4,1)S(1)} %get-tuple-element.10), kind=kOutput, calls=%fused_computation.30 | convolution fusion | flops 4297588736 | bytes 13632000 | tf_op jit(solution)/shard_map/dot_general | solution.py:158
  245.6 52.7 %all_to_all.29 = bf16[4,128,4096]{2,1,0:T(8,128)(2,1)S(1)} all-to-all(bf16[4,128,4096]{2,1,0:T(8,128)(2,1)S(1)} %bitcast.100), channel_id=1, replica_groups=mesh['dp'=32,'tp'=4] {'tp'}, dimensions={0} | all-to-all | bytes 8388608 | tf_op jit(solution)/shard_map/all_to_all | solution.py:23
  (49 shorter events, 12.0 us)
Async XLA Ops:
  0.0 168.6 %copy-start = (bf16[4096,256]{1,0:T(8,128)(2,1)S(1)}, bf16[4096,256]{1,0:T(8,128)(2,1)}, u32[]{:S(2)}) copy-start(bf16[4096,256]{1,0:T(8,128)(2,1)} %param.12) | copy-start | bytes 6291460
  23.1 12.0 %copy-start.4 = (s32[16384]{0:T(1024)S(1)}, s32[16384]{0:T(1024)}, u32[]{:S(2)}) copy-start(s32[16384]{0:T(1024)} %param.15) | copy-start | bytes 196612
  23.1 112.1 %all-to-all-start = ((bf16[128,8,4096]{2,1,0:T(8,128)(2,1)}), bf16[128,8,4096]{2,1,0:T(8,128)(2,1)}, u32[]{:S(2)}, u32[]{:S(2)}) async-start(bf16[128,8,4096]{2,1,0:T(8,128)(2,1)} %bitcast.95), calls=%async_computation | async-start | bytes 16777216 | tf_op jit(solution)/shard_map/all_to_all | solution.py:119
  148.1 1.6 copy-start.3
  168.6 8.3 %copy-start.7 = (f32[2,4,512,1024]{2,3,1,0:T(8,128)S(1)}, f32[2,4,512,1024]{2,3,1,0:T(8,128)}, u32[]{:S(2)}) copy-start(f32[2,4,512,1024]{2,3,1,0:T(8,128)} %get-tuple-element.27) | copy-start | bytes 50331652
  174.6 4.0 %copy-start.5 = (bf16[1024,256]{0,1:T(8,128)(2,1)}, bf16[1024,256]{0,1:T(8,128)(2,1)S(1)}, u32[]{:S(2)}) copy-start(bf16[1024,256]{0,1:T(8,128)(2,1)S(1)} %fusion.30) | copy-start | bytes 1572868
  179.1 11.2 %copy-start.6 = (bf16[1024,256]{0,1:T(8,128)(2,1)S(1)}, bf16[1024,256]{0,1:T(8,128)(2,1)}, u32[]{:S(2)}) copy-start(bf16[1024,256]{0,1:T(8,128)(2,1)} %copy-done.5) | copy-start | bytes 1572868
  199.4 35.8 %all-to-all-start.1 = ((bf16[32,32,1024]{2,1,0:T(8,128)(2,1)}), bf16[32,32,1024]{2,1,0:T(8,128)(2,1)S(1)}, u32[]{:S(2)}, u32[]{:S(2)}) async-start(bf16[32,32,1024]{2,1,0:T(8,128)(2,1)} %bitcast.99), calls=%async_computation.1 | async-start | bytes 4194304 | tf_op jit(solution)/shard_map/all_to_all | solution.py:150
  245.5 55.1 %copy-start.1 = (bf16[4096,256]{1,0:T(8,128)(2,1)S(1)}, bf16[4096,256]{1,0:T(8,128)(2,1)}, u32[]{:S(2)}) copy-start(bf16[4096,256]{1,0:T(8,128)(2,1)} %param.12) | copy-start | bytes 6291460
  298.2 1.2 copy-start.2
where the time goes:
time: 302 us; the launch traced here: 301 us
  waiting for transfers between devices  104 us (34%)
  matrix products  63.7 us (21%)
  blocking collectives  52.7 us (17%)
  other arithmetic  32.1 us (11%)
  local copies, waits for them, and re-layouts  29.9 us (10%)
  starting transfers between devices  17.6 us (6%)
    all_to_all x1, waiting for transfers between devices, body(): lax.all_to_all(fanned.reshape(slot_total, model_width), ('dp', 'tp'), spl...  74.4 us
    all_to_all x1, blocking collectives, sum_at_owner(): lax.all_to_all(pieces, axis, split_axis=0, concat_axis=0, tiled=True)  52.7 us
    all_to_all x1, waiting for transfers between devices, body(): lax.all_to_all(context, 'dp', split_axis=0, concat_axis=0, tiled=True)  30 us
    sub x2, matrix products, attend(): weights = jnp.exp(score_values - row_peak)  22.3 us
    dot_general x1, matrix products, body(): jnp.dot(arrived, w_query, preferred_element_type=jnp.float32)  12.9 us
    all_to_all x1, starting transfers between devices, body(): lax.all_to_all(fanned.reshape(slot_total, model_width), ('dp', 'tp'), spl...  11.9 us
    dot_general x1, local copies, waits for them, and re-layouts, body(): jnp.dot(arrived, w_query, preferred_element_type=jnp.float32)  11.5 us
    dot_general x2, matrix products, attend(): jnp.einsum('kgqs,skd->qkgd', weights, value_heads, preferred_element_type...  8.59 us
  transfers between devices with their start and end apart: 2, of which 2 were waited for; matrix products, arithmetic and copies ran while one was open for 9% of the time, Pallas kernels for 0%

commit v1 on v0

v1 whole, which is shorter than its diff:
```python
import functools

import jax
import jax.numpy as jnp
from jax import lax
from jax.experimental import pallas as pl
from jax.experimental.pallas import tpu as pltpu
from jax.sharding import PartitionSpec as P


HEAD_DIM = 128
NY, NX, NZ = 4, 4, 4
GROUPS = 32
TOK = 128
ROWS = NZ * TOK
TILE = 16
TILES = ROWS // TILE
LOG2E = 1.4426950408889634

rope_base = 500000.0
norm_eps = 1e-05
score_floor = -1e30

AXES = ("dp", "tp")
VMEM = pltpu.VMEM


def group_of(y, x, core):
    return ((y % NY) * NX + (x % NX)) * 2 + core


def pairs(move):
    out = []
    for y in range(NY):
        for x in range(NX):
            for core in range(2):
                for z in range(NZ):
                    y2, x2, core2, z2 = move(y, x, core, z)
                    out.append(
                        (group_of(y, x, core) * NZ + z, group_of(y2, x2, core2) * NZ + z2 % NZ)
                    )
    return out


def first_axis(s):
    return pairs(
        lambda y, x, core, z: (y, x + s, core, z) if core == 0 else (y + s, x, core, z)
    )


def second_axis(s):
    return pairs(
        lambda y, x, core, z: (y + s, x, core, z) if core == 0 else (y, x + s, core, z)
    )


def along_z(s):
    return pairs(lambda y, x, core, z: (y, x, core, z + s))


def send(array, moves):
    return lax.ppermute(array, AXES, moves)


def swap_cores(array):
    return send(array, pairs(lambda y, x, core, z: (y, x, 1 - core, z)))


def cost(flops, nbytes, exps=0):
    return pl.CostEstimate(flops=int(flops), bytes_accessed=int(nbytes), transcendentals=int(exps))


def whole():
    return pl.BlockSpec(memory_space=VMEM)


def scalars():
    return pl.BlockSpec(memory_space=pltpu.SMEM)


def small():
    return pltpu.CompilerParams(vmem_limit_bytes=24 * 2**20)


def norm_kernel(tokens_ref, gain_ref, out_ref):
    gain = gain_ref[...]

    def chunk(i, _):
        at = pl.ds(pl.multiple_of(i * 16, 16), 16)
        rows = tokens_ref[at, :].astype(jnp.float32)
        scale = lax.rsqrt(jnp.mean(rows * rows, axis=1, keepdims=True) + norm_eps)
        out_ref[at, :] = (rows * scale * gain).astype(jnp.bfloat16)
        return 0

    lax.fori_loop(0, tokens_ref.shape[0] // 16, chunk, 0)


def normalise(tokens, gain):
    rows, width = tokens.shape
    return pl.pallas_call(
        norm_kernel,
        out_shape=jax.ShapeDtypeStruct((rows, width), jnp.bfloat16),
        in_specs=[whole(), whole()],
        out_specs=whole(),
        compiler_params=small(),
        cost_estimate=cost(rows * width * 5, rows * width * 4),
    )(tokens, gain.reshape(1, width))


def as_column(row):
    return jnp.broadcast_to(row, (128, 128)).T


def order_kernel(packed_ref, out_ref):
    lane = lax.broadcasted_iota(jnp.int32, (128, 128), 1).astype(jnp.float32)
    blocks = ROWS // 128

    def one_group(g, _):
        row = packed_ref[pl.ds(g, 1), :]
        pieces = [row[:, i * 128 : (i + 1) * 128] for i in range(blocks)]
        sums = [jnp.zeros((128, 128), jnp.float32) for _ in range(blocks)]
        for j in range(blocks):
            column = as_column(pieces[j])
            below = jnp.zeros((128, 128), jnp.float32)
            for i in range(blocks):
                below = below + jnp.where(pieces[i] < column, 1.0, 0.0)
            rank = jnp.sum(below, axis=1, keepdims=True)
            for i in range(blocks):
                sums[i] = sums[i] + jnp.where(rank == lane + float(i * 128), column, 0.0)
        out_ref[pl.ds(g, 1), :] = jnp.concatenate(
            [jnp.sum(s, axis=0, keepdims=True) for s in sums], axis=1
        )
        return 0

    lax.fori_loop(0, GROUPS, one_group, 0)


def order_groups(packed):
    return pl.pallas_call(
        order_kernel,
        out_shape=jax.ShapeDtypeStruct((GROUPS, ROWS), jnp.float32),
        in_specs=[whole()],
        out_specs=whole(),
        compiler_params=small(),
        cost_estimate=cost(6 * GROUPS * ROWS * ROWS, 8 * GROUPS * ROWS),
    )(packed)


def turn(head, cosine, sine):
    return head * cosine + pltpu.roll(head, HEAD_DIM // 2, 1) * sine


def stacked(refs):
    if len(refs) == 1:
        return refs[0][...]
    return jnp.concatenate([ref[...] for ref in refs], axis=0)


def keys_and_values(rows, wk_ref, wv_ref, cosine, sine):
    keys = jnp.dot(rows, wk_ref[...], preferred_element_type=jnp.float32)
    values = jnp.dot(rows, wv_ref[...], preferred_element_type=jnp.float32)
    out = []
    for head in range(2):
        at = slice(head * HEAD_DIM, (head + 1) * HEAD_DIM)
        key = turn(keys[:, at], cosine, sine)
        out.append(jnp.concatenate([key, values[:, at]], axis=1).astype(jnp.bfloat16))
    return out


def kv_kernel(parts, first, *refs):
    wk_ref, wv_ref, cos_ref, sin_ref, out_ref = refs[parts:]
    rows = stacked(refs[:parts])
    at = slice(first, first + rows.shape[0])
    for head, block in enumerate(
        keys_and_values(rows, wk_ref, wv_ref, cos_ref[at, :], sin_ref[at, :])
    ):
        out_ref[head] = block


def project_kv(pieces, w_key, w_value, cosine, sine, first):
    width = w_key.shape[0]
    rows = sum(p.shape[0] for p in pieces)
    return pl.pallas_call(
        functools.partial(kv_kernel, len(pieces), first),
        out_shape=jax.ShapeDtypeStruct((2, rows, 256), jnp.bfloat16),
        in_specs=[whole()] * (len(pieces) + 4),
        out_specs=whole(),
        compiler_params=small(),
        cost_estimate=cost(2 * rows * width * 512, width * 1024 + rows * width * 2),
    )(*pieces, w_key, w_value, cosine, sine)


def sorting(rank_row):
    slot = lax.broadcasted_iota(jnp.int32, (ROWS, ROWS), 0)
    return (slot == rank_row).astype(jnp.bfloat16)


def last_kv_kernel(parts, core_ref, *refs):
    wk_ref, wv_ref, cos_ref, sin_ref, rank_ref = refs[parts : parts + 5]
    done_refs, (other_ref, mine_ref) = refs[parts + 5 : -3], refs[-3:-1]
    last_ref = refs[-1]
    rows = stacked(refs[:parts])
    at = slice(ROWS - rows.shape[0], ROWS)
    for head, block in enumerate(
        keys_and_values(rows, wk_ref, wv_ref, cos_ref[at, :], sin_ref[at, :])
    ):
        last_ref[head] = block
    pick = sorting(rank_ref[...])
    core = core_ref[0]
    for head, out_ref in ((1 - core, other_ref), (core, mine_ref)):
        rows = jnp.concatenate([ref[head] for ref in (*done_refs, last_ref)], axis=0)
        out_ref[...] = jnp.dot(pick, rows, preferred_element_type=jnp.float32).astype(jnp.bfloat16)


def finish_kv(core, pieces, w_key, w_value, cosine, sine, rank_row, done):
    width = w_key.shape[0]
    rows = sum(p.shape[0] for p in pieces)
    shape = jax.ShapeDtypeStruct((ROWS, 256), jnp.bfloat16)
    return pl.pallas_call(
        functools.partial(last_kv_kernel, len(pieces)),
        out_shape=(shape, shape),
        in_specs=[scalars()] + [whole()] * (len(pieces) + 5 + len(done)),
        out_specs=(whole(), whole()),
        scratch_shapes=[pltpu.VMEM((2, rows, 256), jnp.bfloat16)],
        compiler_params=small(),
        cost_estimate=cost(2 * rows * width * 512, width * 1024 + rows * width * 2),
    )(core, *pieces, w_key, w_value, cosine, sine, rank_row, *done)


def q_kernel(parts, core_ref, *refs):
    w_ref, cos_ref, sin_ref, rank_ref, other_ref, mine_ref = refs[parts:]
    both = jnp.dot(stacked(refs[:parts]), w_ref[...], preferred_element_type=jnp.float32)
    cosine, sine = cos_ref[...], sin_ref[...]
    turned = jnp.concatenate(
        [turn(both[:, :HEAD_DIM], cosine, sine), turn(both[:, HEAD_DIM:], cosine, sine)], axis=1
    ).astype(jnp.bfloat16)
    ordered = jnp.dot(
        sorting(rank_ref[...]), turned, preferred_element_type=jnp.float32
    ).astype(jnp.bfloat16)
    step = pl.program_id(0)

    @pl.when(step < 2)
    def _():
        other_ref[...] = ordered

    @pl.when(step >= 2)
    def _():
        mine_ref[...] = ordered


def project_q(core, pieces, w_query, cosine, sine, rank_row):
    width = w_query.shape[0]

    def columns(step, core_ref):
        half = jnp.where(step < 2, 1 - core_ref[0], core_ref[0])
        return (0, half * 2 + step % 2)

    shape = jax.ShapeDtypeStruct((ROWS, 512), jnp.bfloat16)
    return pl.pallas_call(
        functools.partial(q_kernel, len(pieces)),
        out_shape=(shape, shape),
        grid_spec=pltpu.PrefetchScalarGridSpec(
            num_scalar_prefetch=1,
            grid=(4,),
            in_specs=[whole()] * len(pieces)
            + [pl.BlockSpec((width, 256), columns)]
            + [whole()] * 3,
            out_specs=(
                pl.BlockSpec((ROWS, 256), lambda i, s: (0, jnp.minimum(i, 1))),
                pl.BlockSpec((ROWS, 256), lambda i, s: (0, jnp.maximum(i - 2, 0))),
            ),
        ),
        compiler_params=small(),
        cost_estimate=cost(2 * ROWS * width * 1024, width * 2048 + ROWS * width * 2),
    )(core, *pieces, w_query, cosine, sine, rank_row)


def attend_kernel(opening, closing, count, low_ref, high_ref, *refs):
    q_refs, refs = refs[:2], refs[2:]
    key_at_ref, row_at_ref, row_from_ref = refs[:3]
    kv_refs, refs = refs[3 : 3 + count], refs[3 + count :]
    if not opening:
        old_ref, refs = refs[0], refs[1:]
    out_refs, state_ref = refs[:-1], refs[-1]
    scale = HEAD_DIM ** (-0.5) * LOG2E

    def at(u, size):
        return pl.ds(pl.multiple_of(u * size, size), size)

    def queries(u):
        query = jnp.concatenate(
            [
                ref[at(u, TILE), h * HEAD_DIM : (h + 1) * HEAD_DIM]
                for ref in q_refs
                for h in range(4)
            ],
            axis=0,
        )
        return (
            query,
            as_column(row_at_ref[pl.ds(u, 1), :]),
            as_column(row_from_ref[pl.ds(u, 1), :]),
        )

    def keys(t):
        return jnp.concatenate(
            [ref[:, at(t, TILE), :].reshape(-1, 256) for ref in kv_refs], axis=0
        )

    def spread(a, wide=1):
        a = jnp.broadcast_to(a, (128, 128))
        return a if wide == 1 else jnp.concatenate([a] * wide, axis=1)

    def update(bound, kv, key_at, state):
        query, upper, lower = bound
        scores = lax.dot_general(
            query,
            kv[:, :HEAD_DIM],
            (((1,), (1,)), ((), ())),
            preferred_element_type=jnp.float32,
        )
        wide = scores.shape[1] // 128
        allowed = (key_at <= spread(upper, wide)) & (key_at >= spread(lower, wide))
        scores = jnp.where(allowed, scores, score_floor)
        peak = spread(jnp.max(scores, axis=1, keepdims=True))
        if state is not None:
            peak = jnp.maximum(peak, state[0])
        weights = jnp.exp2((scores - spread(peak, wide)) * scale)
        total = spread(jnp.sum(weights, axis=1, keepdims=True))
        mixed = jnp.dot(
            weights.astype(jnp.bfloat16), kv[:, HEAD_DIM:], preferred_element_type=jnp.float32
        )
        if state is not None:
            keep = jnp.exp2((state[0] - peak) * scale)
            total = total + state[1] * keep
            mixed = mixed + state[2] * keep
        return peak, total, mixed

    def load(ref, u):
        return tuple(ref[at(u, 128), i * 128 : (i + 1) * 128] for i in range(3))

    def save(u, state):
        for i, part in enumerate(state):
            state_ref[at(u, 128), i * 128 : (i + 1) * 128] = part

    def write(u, state):
        _, total, mixed = state
        context = (mixed / total).astype(jnp.bfloat16)
        for i, ref in enumerate(out_refs):
            for h in range(4):
                block = (i * 4 + h) * TILE
                ref[at(u, TILE), h * HEAD_DIM : (h + 1) * HEAD_DIM] = context[block : block + TILE]

    def start(u):
        low, high = low_ref[u], high_ref[u]
        t0 = jnp.minimum(low, TILES - 1)
        t1 = jnp.minimum(low + 1, TILES - 1)
        at0 = jnp.where(low < high, key_at_ref[pl.ds(t0, 1), :], -1.0)
        at1 = jnp.where(low + 1 < high, key_at_ref[pl.ds(t1, 1), :], -1.0)
        kv = jnp.concatenate([keys(t0), keys(t1)], axis=0)
        state = None if opening else load(old_ref, u)
        state = update(queries(u), kv, jnp.concatenate([at0, at1], axis=1), state)
        save(u, state)
        if closing:
            write(u, state)

    def two(i, _):
        start(2 * i)
        start(2 * i + 1)
        return 0

    lax.fori_loop(0, TILES // 2, two, 0)

    def rest(u, _):
        def more(t, _):
            state = update(
                queries(u), keys(t), key_at_ref[pl.ds(t, 1), :], load(state_ref, u)
            )
            save(u, state)
            if closing:
                write(u, state)
            return 0

        return lax.fori_loop(low_ref[u] + 2, high_ref[u], more, 0)

    lax.fori_loop(0, TILES, rest, 0)


def attend(bounds, queries, key_at, rows_bounds, kvs, state, closing):
    opening = state is None
    running = jax.ShapeDtypeStruct((TILES * 128, 384), jnp.float32)
    context = [jax.ShapeDtypeStruct((ROWS, 512), jnp.bfloat16)] * 2
    operands = [*bounds, *queries, key_at, *rows_bounds, *kvs, *(() if opening else (state,))]
    rows = sum(kv.shape[0] for kv in kvs) * TILE * 2
    return pl.pallas_call(
        functools.partial(attend_kernel, opening, closing, len(kvs)),
        out_shape=context if closing else running,
        in_specs=[scalars(), scalars()] + [whole()] * (len(operands) - 2),
        out_specs=[whole()] * 2 if closing else whole(),
        scratch_shapes=[pltpu.VMEM((TILES * 128, 384), jnp.float32)] if closing else (),
        compiler_params=pltpu.CompilerParams(vmem_limit_bytes=32 * 2**20),
        cost_estimate=cost(TILES * 128 * rows * 512, 10e6, TILES * 128 * rows),
    )(*operands)


def unsort(rank_row, block, parts):
    slot = lax.broadcasted_iota(jnp.int32, (TOK, ROWS), 1)
    rank = as_column(rank_row[:, block * TOK : (block + 1) * TOK])
    pick = (slot == jnp.concatenate([rank] * (ROWS // 128), axis=1)).astype(jnp.bfloat16)
    return [
        jnp.dot(pick, part[...], preferred_element_type=jnp.float32).astype(jnp.bfloat16)
        for part in parts
    ]


def product_kernel(wanted, core_ref, rank_ref, mine_ref, other_ref, w_ref, *out_refs):
    core = core_ref[0]
    mine_at = pl.ds(pl.multiple_of(core * 512, 512), 512)
    other_at = pl.ds(pl.multiple_of((1 - core) * 512, 512), 512)
    half = w_ref.shape[1] // 2
    rank = rank_ref[...]
    rows = {}
    for block, side in wanted:
        if block not in rows:
            rows[block] = unsort(rank, block, (mine_ref, other_ref))
    for side in range(2):
        group = [(i, block) for i, (block, s) in enumerate(wanted) if s == side]
        mine = jnp.concatenate([rows[block][0] for _, block in group], axis=0)
        other = jnp.concatenate([rows[block][1] for _, block in group], axis=0)
        for at in range(side * half, (side + 1) * half, 1024):
            product = jnp.dot(
                mine, w_ref[mine_at, at : at + 1024], preferred_element_type=jnp.float32
            ) + jnp.dot(other, w_ref[other_at, at : at + 1024], preferred_element_type=jnp.float32)
            for n, (i, _) in enumerate(group):
                out_refs[i][:, at - side * half : at - side * half + 1024] = product[
                    n * TOK : (n + 1) * TOK
                ].astype(jnp.bfloat16)


def products(core, rank_row, mine, other, w_output, wanted):
    width = w_output.shape[1]
    shape = jax.ShapeDtypeStruct((TOK, width // 2), jnp.bfloat16)
    return pl.pallas_call(
        functools.partial(product_kernel, wanted),
        out_shape=[shape] * len(wanted),
        in_specs=[scalars()] + [whole()] * 4,
        out_specs=[whole()] * len(wanted),
        compiler_params=small(),
        cost_estimate=cost(TOK * 1024 * width * len(wanted), 1024 * width * 2),
    )(core, rank_row, mine, other, w_output)


def document_start(position, starts):
    reached = starts <= position[..., None]
    return jnp.max(jnp.where(reached, starts, 0), axis=-1)


def layer(tokens, norm_gain, w_query, w_key, w_value, w_output, doc_lengths, pack_index):
    group = lax.axis_index("dp")
    z = lax.axis_index("tp")
    core = group % 2
    chip_x = (group // 2) % NX
    chip_y = group // (2 * NX)
    core_arg = core.astype(jnp.int32).reshape(1)

    normed = normalise(tokens, norm_gain)
    below = send(normed, along_z(1))
    above = send(normed, along_z(-1))
    far_low = send(below[: TOK // 2], along_z(1))
    far_high = send(above[TOK // 2 :], along_z(-1))

    number = jnp.arange(doc_lengths.shape[0], dtype=jnp.int32)
    starts = jnp.sum(jnp.where(number[None, :] < number[:, None], doc_lengths[None, :], 0), axis=1)
    by_group = pack_index.reshape(GROUPS, NZ, TOK)
    own = lax.dynamic_index_in_dim(by_group, group, 0, keepdims=False)
    order = (z + jnp.array([0, NZ - 1, 1, 2], jnp.int32)) % NZ
    packed = jnp.take(own, order, axis=0).reshape(ROWS)
    place = packed - document_start(packed, starts)
    rank_row = jnp.sum((packed[:, None] < packed[None, :]).astype(jnp.int32), axis=0)
    rank_row = rank_row.reshape(1, ROWS)
    half_dim = HEAD_DIM // 2
    frequency = rope_base ** (-2.0 * jnp.arange(half_dim, dtype=jnp.float32) / HEAD_DIM)
    angles = place.astype(jnp.float32)[:, None] * frequency[None, :]
    cosine, sine = jnp.cos(angles), jnp.sin(angles)
    cosine = jnp.concatenate([cosine, cosine], axis=1)
    sine = jnp.concatenate([-sine, sine], axis=1)

    kv_own = project_kv((normed,), w_key, w_value, cosine, sine, 0)
    kv_near = project_kv((below, above), w_key, w_value, cosine, sine, TOK)
    kv_other, kv_mine = finish_kv(
        core_arg, (far_low, far_high), w_key, w_value, cosine, sine, rank_row, (kv_own, kv_near)
    )
    kv_partner = swap_cores(kv_other)
    chip = jnp.concatenate([kv_mine[None], kv_partner[None]], axis=0)

    back = send(chip, first_axis(1))
    ahead = send(chip, first_axis(-1))
    far_a = send(back[:1], first_axis(1))
    far_b = send(ahead[1:], first_axis(-1))
    line_a = jnp.concatenate([chip, back], axis=0)
    a_back = send(line_a, second_axis(1))
    a_ahead = send(line_a, second_axis(-1))
    line_b = jnp.concatenate([ahead, far_a, far_b], axis=0)
    b_ahead = send(line_b, second_axis(-1))
    b_back = send(line_b, second_axis(1))
    a_far = send(a_back, second_axis(1))
    b_far = send(b_ahead, second_axis(-1))

    q_other, q_mine = project_q(
        core_arg, (normed, below, above, far_low, far_high), w_query, cosine, sine, rank_row
    )
    q_partner = swap_cores(q_other)
    queries = (q_mine, q_partner)

    ordered = order_groups(pack_index.reshape(GROUPS, ROWS).astype(jnp.float32))
    offsets = jnp.array([0, -1, 1, 2], jnp.int32)
    outer, inner = offsets[:, None, None], offsets[None, :, None]
    which = (core + jnp.arange(2, dtype=jnp.int32)) % 2
    dy = jnp.where(core == 0, outer, inner)
    dx = jnp.where(core == 0, inner, outer)
    source = (((chip_y + dy) % NY) * NX + (chip_x + dx) % NX) * 2 + which[None, None, :]
    key_at = jnp.take(ordered, source.reshape(GROUPS), axis=0)
    key_at = key_at.reshape(GROUPS, TILES, TILE).transpose(1, 0, 2)
    rows_at = jnp.take(ordered, jnp.stack([group, group + 1 - 2 * core]), axis=0)
    rows_from = document_start(rows_at, starts.astype(jnp.float32))
    rows_at = rows_at.reshape(2, TILES, TILE)
    rows_from = rows_from.reshape(2, TILES, TILE)
    first_needed = jnp.min(rows_from, axis=(0, 2))
    last_needed = jnp.max(rows_at, axis=(0, 2))

    def per_row(a):
        a = jnp.broadcast_to(a.transpose(1, 0, 2)[:, :, None, :], (TILES, 2, 4, TILE))
        return a.reshape(TILES, 128)

    rows_bounds = (per_row(rows_at), per_row(rows_from))
    state = None
    for name, first, count, kvs in (
        ("att_one", 0, 8, (line_a, line_b)),
        ("att_two", 8, 16, (a_back, b_back, a_ahead, b_ahead)),
        ("att_end", 24, 8, (a_far, b_far)),
    ):
        part = key_at[:, first : first + count].reshape(TILES, count * TILE)
        tile_first = jnp.min(part, axis=1)
        tile_last = jnp.max(part, axis=1)
        low = jnp.sum((tile_last[None, :] < first_needed[:, None]).astype(jnp.int32), axis=1)
        high = jnp.sum((tile_first[None, :] <= last_needed[:, None]).astype(jnp.int32), axis=1)
        state = attend(
            (low, high), queries, part, rows_bounds, kvs, state, name == "att_end"
        )
    mine, partner = state
    other = swap_cores(partner)

    p, q = products(core_arg, rank_row, mine, other, w_output, ((1, 0), (2, 1)))
    p, q = send(p, along_z(1)), send(q, along_z(-1))
    p1, q1, p2, q2, p3, q3 = products(
        core_arg,
        rank_row,
        mine,
        other,
        w_output,
        ((3, 0), (3, 1), (2, 0), (1, 1), (0, 0), (0, 1)),
    )

    def plus(a, b):
        return a.astype(jnp.float32) + b.astype(jnp.float32)

    p = send(plus(p, p1).astype(jnp.bfloat16), along_z(1))
    q = send(plus(q, q1).astype(jnp.bfloat16), along_z(-1))
    p = send(plus(p, p2).astype(jnp.bfloat16), along_z(1))
    q = send(plus(q, q2).astype(jnp.bfloat16), along_z(-1))
    attended = jnp.concatenate([plus(p, p3), plus(q, q3)], axis=1)
    return (tokens.astype(jnp.float32) + attended).astype(jnp.bfloat16)


def solution(mesh):
    placed = (
        P(("dp", "tp"), None),
        P(),
        P(None, "tp"),
        P(None, "tp"),
        P(None, "tp"),
        P("tp", None),
        P(),
        P(),
    )
    return jax.shard_map(
        layer, mesh=mesh, in_specs=placed, out_specs=P(("dp", "tp"), None), check_vma=False
    )
```

time: 302 us -> 210 us (0.70)
  Pallas kernels: 0 us -> 75.7 us
  matrix products: 63.7 us -> 0 us
  blocking collectives: 52.7 us -> 0 us
  waiting for transfers between devices: 104 us -> 71.5 us
  other arithmetic: 32.1 us -> 7.34 us
  starting transfers between devices: 17.6 us -> 36 us
  local copies, waits for them, and re-layouts: 29.9 us -> 18.5 us
    all_to_all x2 -> x0, waiting for transfers between devices: 104 us -> none  [the longest x1 74.4 us: body(): lax.all_to_all(fanned.reshape(slot_total, model_width), ('dp', 'tp'), spl...]
    pallas_call x0 -> x11, Pallas kernels: none -> 75.7 us  [the longest x3 38.3 us: attend(): pl.pallas_call(functools.partial(attend_kernel, opening, closing, len(kvs...]
    ppermute x0 -> x23, waiting for transfers between devices: none -> 71.5 us  [send(): return lax.ppermute(array, AXES, moves)]
    all_to_all x1 -> x0, blocking collectives: 52.7 us -> none  [sum_at_owner(): lax.all_to_all(pieces, axis, split_axis=0, concat_axis=0, tiled=True)]
    dot_general x6 -> x0, matrix products: 41.4 us -> none  [the longest x1 12.9 us: body(): jnp.dot(arrived, w_query, preferred_element_type=jnp.float32)]
    ppermute x0 -> x23, starting transfers between devices: none -> 36 us  [send(): return lax.ppermute(array, AXES, moves)]
    sub x2 -> x0, matrix products: 22.3 us -> none  [attend(): weights = jnp.exp(score_values - row_peak)]
    all_to_all x2 -> x0, starting transfers between devices: 17.6 us -> none  [the longest x1 11.9 us: body(): lax.all_to_all(fanned.reshape(slot_total, model_width), ('dp', 'tp'), spl...]
  transfers between devices with their start and end apart: 2 -> 23, of which waited for: 2 -> 10; matrix products, arithmetic and copies ran while one was open for 9% -> 7% of each run, Pallas kernels for 0% -> 27%
where the time goes in v1:
time: 210 us
  Pallas kernels  75.7 us (36%)
  waiting for transfers between devices  71.5 us (34%)
  starting transfers between devices  36 us (17%)
  local copies, waits for them, and re-layouts  18.5 us (9%)
  other arithmetic  7.34 us (3%)
    ppermute x23, waiting for transfers between devices, send(): return lax.ppermute(array, AXES, moves)  71.5 us
    pallas_call x3, Pallas kernels, attend(): pl.pallas_call(functools.partial(attend_kernel, opening, closing, len(kvs...  38.3 us
    ppermute x23, starting transfers between devices, send(): return lax.ppermute(array, AXES, moves)  36 us
    pallas_call x1, Pallas kernels, project_q(): pl.pallas_call(functools.partial(q_kernel, len(pieces)), out_shape=(shape...  11 us
    unnamed x36, local copies, waits for them, and re-layouts  10.6 us
    pallas_call x1, Pallas kernels, order_groups(): pl.pallas_call(order_kernel, out_shape=jax.ShapeDtypeStruct((GROUPS, ROWS...  10.6 us
    pallas_call x2, Pallas kernels, products(): pl.pallas_call(functools.partial(product_kernel, wanted), out_shape=[shap...  5.67 us
    pallas_call x2, Pallas kernels, project_kv(): pl.pallas_call(functools.partial(kv_kernel, len(pieces), first), out_shap...  5.06 us
  transfers between devices with their start and end apart: 23, of which 10 were waited for; matrix products, arithmetic and copies ran while one was open for 7% of the time, Pallas kernels for 27%

profile of v1, /device:TPU:0, one launch (start us, length us, event | category | flops | bytes accessed | tf_op | source)
XLA Modules:
  0.0 209.6 jit_solution(7899559284226554330)
XLA Ops:
  10.6 21.2 %collective-permute-done.refs_1_.refs_0_ = bf16[128,4096]{1,0:T(8,128)(2,1)} collective-permute-done((bf16[128,4096]{1,0:T(8,128)(2,1)}, bf16[128,4096]{1,0:T(8,128)(2,1)}, u32[]{:S(2)}, u32[]{:S(2)}) %collective-permute-start) | collective-permute-done | bytes 1048608 | tf_op jit(solution)/shard_map/ppermute | solution.py:62
  35.6 3.2 %collective-permute-start.3 = (bf16[64,4096]{1,0:T(8,128)(2,1)}, bf16[64,4096]{1,0:T(8,128)(2,1)}, u32[]{:S(2)}, u32[]{:S(2)}) collective-permute-start(bf16[64,4096]{1,0:T(8,128)(2,1)} %slice.36), channel_id=1, source_target_pairs={{0,3},{1,0},{2,1},{3,2},{4,7},{5,4},{6,5},{7,6},{8,11},{9,8},{10,9... | collective-permute-start | bytes 1572872 | tf_op jit(solution)/shard_map/ppermute | solution.py:62
  42.9 2.9 %shard_map.104.refs_8_ = bf16[2,256,256]{2,1,0:T(8,128)(2,1)S(1)} custom-call(bf16[128,4096]{1,0:T(8,128)(2,1)} %collective-permute-done.refs_1_.refs_0_, bf16[128,4096]{1,0:T(8,128)(2,1)} %collective-permute-done.1.refs_2_.refs_1_, bf16[4096,256]{1,0:T(8,128)(2,1)S(1)} %copy-done, bf16[4096,256]{1,0:T(8,128)(2,1)S(1)} %copy-done.2, ...), custom_call_target="tpu_custom_call" | custom-call | flops 1073741824 | bytes 6291456 | tf_op jit(solution)/shard_map/pallas_call | solution.py:183
  45.8 2.4 %collective-permute-done.2.refs_3_.refs_0_ = bf16[64,4096]{1,0:T(8,128)(2,1)S(1)} collective-permute-done((bf16[64,4096]{1,0:T(8,128)(2,1)}, bf16[64,4096]{1,0:T(8,128)(2,1)S(1)}, u32[]{:S(2)}, u32[]{:S(2)}) %collective-permute-start.2) | collective-permute-done | bytes 524320 | tf_op jit(solution)/shard_map/ppermute | solution.py:62
  49.4 2.9 %shard_map.105 = (bf16[512,256]{1,0:T(8,128)(2,1)}, bf16[512,256]{1,0:T(8,128)(2,1)S(1)}) custom-call(s32[1]{0:T(128)} %bitcast.core_ref, bf16[64,4096]{1,0:T(8,128)(2,1)S(1)} %collective-permute-done.2.refs_3_.refs_0_, bf16[64,4096]{1,0:T(8,128)(2,1)} %collective-permute-done.3.refs_4_.refs_1_, bf16[4096,256]{1,0:T(8,128)(2,1)S(1)} %copy-done, ...), custom_call_target="tpu_custom_call" | custom-call | flops 536870912 | bytes 5242880 | tf_op jit(solution)/shard_map/pallas_call | solution.py:219
  54.1 2.8 %collective-permute-start.9 = (bf16[2,512,256]{2,1,0:T(8,128)(2,1)S(1)}, bf16[2,512,256]{2,1,0:T(8,128)(2,1)S(1)}, u32[]{:S(2)}, u32[]{:S(2)}) collective-permute-start(bf16[2,512,256]{2,1,0:T(8,128)(2,1)S(1)} %pad_maximum_fusion.1), channel_id=1, source_target_pairs={{0,24},{1,25},{2,26},{3,27},{4,100},{5,101},{6,102},{7,103},{8,0},... | collective-permute-start | bytes 1572872 | tf_op jit(solution)/shard_map/ppermute | solution.py:62
  57.0 10.4 %collective-permute-done.6 = bf16[2,512,256]{2,1,0:T(8,128)(2,1)S(1)} collective-permute-done((bf16[2,512,256]{2,1,0:T(8,128)(2,1)S(1)}, bf16[2,512,256]{2,1,0:T(8,128)(2,1)S(1)}, u32[]{:S(2)}, u32[]{:S(2)}) %collective-permute-start.6) | collective-permute-done | bytes 524320 | tf_op jit(solution)/shard_map/ppermute | solution.py:62
  67.5 3.3 %collective-permute-start.11 = (bf16[1,512,256]{2,1,0:T(8,128)(2,1)S(1)}, bf16[1,512,256]{2,1,0:T(8,128)(2,1)S(1)}, u32[]{:S(2)}, u32[]{:S(2)}) collective-permute-start(bf16[1,512,256]{2,1,0:T(8,128)(2,1)S(1)} %slice.38), channel_id=1, source_target_pairs={{0,24},{1,25},{2,26},{3,27},{4,100},{5,101},{6,102},{7,103},{8,0},... | collective-permute-start | bytes 786440 | tf_op jit(solution)/shard_map/ppermute | solution.py:62
  73.4 3.2 %collective-permute-done.10 = bf16[1,512,256]{2,1,0:T(8,128)(2,1)S(1)} collective-permute-done((bf16[1,512,256]{2,1,0:T(8,128)(2,1)S(1)}, bf16[1,512,256]{2,1,0:T(8,128)(2,1)S(1)}, u32[]{:S(2)}, u32[]{:S(2)}) %collective-permute-start.10) | collective-permute-done | bytes 262176 | tf_op jit(solution)/shard_map/ppermute | solution.py:62
  78.1 4.3 %collective-permute-start.12 = (bf16[4,512,256]{2,1,0:T(8,128)(2,1)}, bf16[4,512,256]{2,1,0:T(8,128)(2,1)}, u32[]{:S(2)}, u32[]{:S(2)}) collective-permute-start(bf16[4,512,256]{2,1,0:T(8,128)(2,1)} %constant_dynamic-update-slice_fusion.refs_6_), channel_id=1, source_target_pairs={{0,96},{1,97},{2,98},{3,99},{4,28},{5,29},{6,30},{7,31},{8,104},{9... | collective-permute-start | bytes 3145736 | tf_op jit(solution)/shard_map/ppermute | solution.py:62
  82.3 10.6 %shard_map.100 = f32[32,512]{1,0:T(8,128)S(1)} custom-call(f32[32,512]{1,0:T(8,128)S(1)} %convert_element_type.99.packed_ref), custom_call_target="tpu_custom_call" | custom-call | flops 50331648 | bytes 131072 | tf_op jit(solution)/shard_map/pallas_call | solution.py:139
  97.7 3.2 %collective-permute-start.13 = (bf16[4,512,256]{2,1,0:T(8,128)(2,1)}, bf16[4,512,256]{2,1,0:T(8,128)(2,1)}, u32[]{:S(2)}, u32[]{:S(2)}) collective-permute-start(bf16[4,512,256]{2,1,0:T(8,128)(2,1)} %collective-permute-done.12.refs_8_), channel_id=1, source_target_pairs={{0,96},{1,97},{2,98},{3,99},{4,28},{5,29},{6,30},{7,31},{8,104},{9... | collective-permute-start | bytes 3145736 | tf_op jit(solution)/shard_map/ppermute | solution.py:62
  100.9 3.4 %copy-done.10 = bf16[4096,1024]{1,0:T(8,128)(2,1)S(1)} copy-done((bf16[4096,1024]{1,0:T(8,128)(2,1)S(1)}, bf16[4096,1024]{1,0:T(8,128)(2,1)}, u32[]{:S(2)}) %copy-start.10) | copy-done | bytes 8388632
  104.3 11.0 %shard_map.102 = (bf16[512,512]{1,0:T(8,128)(2,1)}, bf16[512,512]{1,0:T(8,128)(2,1)S(1)}) custom-call(s32[1]{0:T(128)} %bitcast.core_ref, bf16[128,4096]{1,0:T(8,128)(2,1)} %shard_map.101.refs_0_, bf16[128,4096]{1,0:T(8,128)(2,1)} %collective-permute-done.refs_1_.refs_0_, bf16[128,4096]{1,0:T(8,128)(2,1)} %collective-permute-done.1.refs_2_.refs_1_, ...), custom_call_target="tpu_custom_call" | custom-call | flops 4294967296 | bytes 12582912 | tf_op jit(solution)/shard_map/pallas_call | solution.py:259
  118.5 12.0 %shard_map.106.refs_9_ = f32[4096,384]{1,0:T(8,128)S(1)} custom-call(s32[32]{0:T(128)S(1)} %get-tuple-element.42.low_ref, s32[32]{0:T(128)S(1)} %get-tuple-element.39.high_ref, bf16[512,512]{1,0:T(8,128)(2,1)S(1)} %get-tuple-element.19.refs_0_, bf16[512,512]{1,0:T(8,128)(2,1)S(1)} %collective-permute-done.4.refs_1_, f32[32,128]{1,0:T(8,128)S(1)} %copy.34.refs_2_, ...), custom_call_target="tpu_custom_call" | custom-call | flops 536870912 | bytes 10000000 | tf_op jit(solution)/shard_map/pallas_call | solution.py:395
  131.7 14.1 %shard_map.107.refs_7_ = f32[4096,384]{1,0:T(8,128)S(1)} custom-call(s32[32]{0:T(128)S(1)} %get-tuple-element.43.low_ref, s32[32]{0:T(128)S(1)} %get-tuple-element.40.high_ref, bf16[512,512]{1,0:T(8,128)(2,1)S(1)} %get-tuple-element.19.refs_0_, bf16[512,512]{1,0:T(8,128)(2,1)S(1)} %copy-done.4, f32[32,256]{1,0:T(8,128)S(1)} %copy.37.refs_2_, ...), custom_call_target="tpu_custom_call" | custom-call | flops 1073741824 | bytes 10000000 | tf_op jit(solution)/shard_map/pallas_call | solution.py:395
  145.8 12.2 %shard_map.108 = (bf16[512,512]{1,0:T(8,128)(2,1)S(1)}, bf16[512,512]{1,0:T(8,128)(2,1)S(1)}) custom-call(s32[32]{0:T(128)S(1)} %get-tuple-element.44.low_ref, s32[32]{0:T(128)S(1)} %get-tuple-element.41.high_ref, bf16[512,512]{1,0:T(8,128)(2,1)S(1)} %get-tuple-element.19.refs_0_, bf16[512,512]{1,0:T(8,128)(2,1)S(1)} %copy-done.4, ...), custom_call_target="tpu_custom_call" | custom-call | flops 536870912 | bytes 10000000 | tf_op jit(solution)/shard_map/pallas_call | solution.py:395
  162.3 3.3 %collective-permute-start.20 = (bf16[128,2048]{1,0:T(8,128)(2,1)S(1)}, bf16[128,2048]{1,0:T(8,128)(2,1)S(1)}, u32[]{:S(2)}, u32[]{:S(2)}) collective-permute-start(bf16[128,2048]{1,0:T(8,128)(2,1)S(1)} %get-tuple-element.29), channel_id=1, source_target_pairs={{0,3},{1,0},{2,1},{3,2},{4,7},{5,4},{6,5},{7,6},{8,11},{9,8},{10,9... | collective-permute-start | bytes 1572872 | tf_op jit(solution)/shard_map/ppermute | solution.py:62
  165.6 4.1 %shard_map.110 = (bf16[128,2048]{1,0:T(8,128)(2,1)S(1)}, bf16[128,2048]{1,0:T(8,128)(2,1)S(1)}, bf16[128,2048]{1,0:T(8,128)(2,1)S(1)}, bf16[128,2048]{1,0:T(8,12...) custom-call(s32[1]{0:T(128)} %bitcast.core_ref, s32[1,512]{1,0:T(1,128)S(1)} %bitcast.36, ...), custom_call_target="tpu_custom_call" | custom-call | flops 3221225472 | bytes 8388608 | tf_op jit(solution)/shard_map/pallas_call | solution.py:443
  169.6 8.3 %collective-permute-done.17 = bf16[128,2048]{1,0:T(8,128)(2,1)S(1)} collective-permute-done((bf16[128,2048]{1,0:T(8,128)(2,1)S(1)}, bf16[128,2048]{1,0:T(8,128)(2,1)S(1)}, u32[]{:S(2)}, u32[]{:S(2)}) %collective-permute-start.17) | collective-permute-done | bytes 524320 | tf_op jit(solution)/shard_map/ppermute | solution.py:62
  178.3 3.3 %collective-permute-start.21 = (bf16[128,2048]{1,0:T(8,128)(2,1)S(1)}, bf16[128,2048]{1,0:T(8,128)(2,1)S(1)}, u32[]{:S(2)}, u32[]{:S(2)}) collective-permute-start(bf16[128,2048]{1,0:T(8,128)(2,1)S(1)} %add_convert_fusion.1), channel_id=1, source_target_pairs={{0,3},{1,0},{2,1},{3,2},{4,7},{5,4},{6,5},{7,6},{8,11},{9,8},{10,9... | collective-permute-start | bytes 1572872 | tf_op jit(solution)/shard_map/ppermute | solution.py:62
  181.6 11.4 %collective-permute-done.18 = bf16[128,2048]{1,0:T(8,128)(2,1)S(1)} collective-permute-done((bf16[128,2048]{1,0:T(8,128)(2,1)S(1)}, bf16[128,2048]{1,0:T(8,128)(2,1)S(1)}, u32[]{:S(2)}, u32[]{:S(2)}) %collective-permute-start.18) | collective-permute-done | bytes 524320 | tf_op jit(solution)/shard_map/ppermute | solution.py:62
  193.3 3.3 %collective-permute-start.22 = (bf16[128,2048]{1,0:T(8,128)(2,1)S(1)}, bf16[128,2048]{1,0:T(8,128)(2,1)S(1)}, u32[]{:S(2)}, u32[]{:S(2)}) collective-permute-start(bf16[128,2048]{1,0:T(8,128)(2,1)S(1)} %add_convert_fusion), channel_id=1, source_target_pairs={{0,3},{1,0},{2,1},{3,2},{4,7},{5,4},{6,5},{7,6},{8,11},{9,8},{10,9... | collective-permute-start | bytes 1572872 | tf_op jit(solution)/shard_map/ppermute | solution.py:62
  196.6 10.5 %collective-permute-done.19 = bf16[128,2048]{1,0:T(8,128)(2,1)S(1)} collective-permute-done((bf16[128,2048]{1,0:T(8,128)(2,1)S(1)}, bf16[128,2048]{1,0:T(8,128)(2,1)S(1)}, u32[]{:S(2)}, u32[]{:S(2)}) %collective-permute-start.19) | collective-permute-done | bytes 524320 | tf_op jit(solution)/shard_map/ppermute | solution.py:62
  (139 shorter events, 42.0 us)
Async XLA Ops:
  4.2 27.6 %collective-permute-start = (bf16[128,4096]{1,0:T(8,128)(2,1)}, bf16[128,4096]{1,0:T(8,128)(2,1)}, u32[]{:S(2)}, u32[]{:S(2)}) collective-permute-start(bf16[128,4096]{1,0:T(8,128)(2,1)} %shard_map.101.refs_0_), channel_id=1, source_target_pairs={{0,1},{1,2},{2,3},{3,0},{4,5},{5,6},{6,7},{7,4},{8,9},{9,10},{10,1... | collective-permute-start | bytes 3145736 | tf_op jit(solution)/shard_map/ppermute | solution.py:62
  6.2 27.5 %collective-permute-start.1 = (bf16[128,4096]{1,0:T(8,128)(2,1)}, bf16[128,4096]{1,0:T(8,128)(2,1)}, u32[]{:S(2)}, u32[]{:S(2)}) collective-permute-start(bf16[128,4096]{1,0:T(8,128)(2,1)} %shard_map.101.refs_0_), channel_id=1, source_target_pairs={{0,3},{1,0},{2,1},{3,2},{4,7},{5,4},{6,5},{7,6},{8,11},{9,8},{10,9... | collective-permute-start | bytes 3145736 | tf_op jit(solution)/shard_map/ppermute | solution.py:62
  33.7 14.5 %collective-permute-start.2 = (bf16[64,4096]{1,0:T(8,128)(2,1)}, bf16[64,4096]{1,0:T(8,128)(2,1)S(1)}, u32[]{:S(2)}, u32[]{:S(2)}) collective-permute-start(bf16[64,4096]{1,0:T(8,128)(2,1)} %slice.35), channel_id=1, source_target_pairs={{0,1},{1,2},{2,3},{3,0},{4,5},{5,6},{6,7},{7,4},{8,9},{9,10},{10,1... | collective-permute-start | bytes 1572872 | tf_op jit(solution)/shard_map/ppermute | solution.py:62
  35.6 13.9 %collective-permute-start.3 = (bf16[64,4096]{1,0:T(8,128)(2,1)}, bf16[64,4096]{1,0:T(8,128)(2,1)}, u32[]{:S(2)}, u32[]{:S(2)}) collective-permute-start(bf16[64,4096]{1,0:T(8,128)(2,1)} %slice.36), channel_id=1, source_target_pairs={{0,3},{1,0},{2,1},{3,2},{4,7},{5,4},{6,5},{7,6},{8,11},{9,8},{10,9... | collective-permute-start | bytes 1572872 | tf_op jit(solution)/shard_map/ppermute | solution.py:62
  52.3 1.7 collective-permute-start.5
  54.1 13.3 %collective-permute-start.9 = (bf16[2,512,256]{2,1,0:T(8,128)(2,1)S(1)}, bf16[2,512,256]{2,1,0:T(8,128)(2,1)S(1)}, u32[]{:S(2)}, u32[]{:S(2)}) collective-permute-start(bf16[2,512,256]{2,1,0:T(8,128)(2,1)S(1)} %pad_maximum_fusion.1), channel_id=1, source_target_pairs={{0,24},{1,25},{2,26},{3,27},{4,100},{5,101},{6,102},{7,103},{8,0},... | collective-permute-start | bytes 1572872 | tf_op jit(solution)/shard_map/ppermute | solution.py:62
  56.9 10.4 %collective-permute-start.6 = (bf16[2,512,256]{2,1,0:T(8,128)(2,1)S(1)}, bf16[2,512,256]{2,1,0:T(8,128)(2,1)S(1)}, u32[]{:S(2)}, u32[]{:S(2)}) collective-permute-start(bf16[2,512,256]{2,1,0:T(8,128)(2,1)S(1)} %pad_maximum_fusion.1), channel_id=1, source_target_pairs={{0,8},{1,9},{2,10},{3,11},{4,36},{5,37},{6,38},{7,39},{8,16},{9,17... | collective-permute-start | bytes 1572872 | tf_op jit(solution)/shard_map/ppermute | solution.py:62
  67.3 9.2 %collective-permute-start.10 = (bf16[1,512,256]{2,1,0:T(8,128)(2,1)S(1)}, bf16[1,512,256]{2,1,0:T(8,128)(2,1)S(1)}, u32[]{:S(2)}, u32[]{:S(2)}) collective-permute-start(bf16[1,512,256]{2,1,0:T(8,128)(2,1)S(1)} %slice.37), channel_id=1, source_target_pairs={{0,8},{1,9},{2,10},{3,11},{4,36},{5,37},{6,38},{7,39},{8,16},{9,17... | collective-permute-start | bytes 786440 | tf_op jit(solution)/shard_map/ppermute | solution.py:62
  67.5 9.8 %collective-permute-start.11 = (bf16[1,512,256]{2,1,0:T(8,128)(2,1)S(1)}, bf16[1,512,256]{2,1,0:T(8,128)(2,1)S(1)}, u32[]{:S(2)}, u32[]{:S(2)}) collective-permute-start(bf16[1,512,256]{2,1,0:T(8,128)(2,1)S(1)} %slice.38), channel_id=1, source_target_pairs={{0,24},{1,25},{2,26},{3,27},{4,100},{5,101},{6,102},{7,103},{8,0},... | collective-permute-start | bytes 786440 | tf_op jit(solution)/shard_map/ppermute | solution.py:62
  70.8 26.7 %collective-permute-start.7 = (bf16[4,512,256]{2,1,0:T(8,128)(2,1)S(1)}, bf16[4,512,256]{2,1,0:T(8,128)(2,1)}, u32[]{:S(2)}, u32[]{:S(2)}) collective-permute-start(bf16[4,512,256]{2,1,0:T(8,128)(2,1)S(1)} %pad_maximum_fusion.refs_5_), channel_id=1, source_target_pairs={{0,32},{1,33},{2,34},{3,35},{4,12},{5,13},{6,14},{7,15},{8,40},{9,... | collective-permute-start | bytes 3145736 | tf_op jit(solution)/shard_map/ppermute | solution.py:62
  78.1 19.6 %collective-permute-start.12 = (bf16[4,512,256]{2,1,0:T(8,128)(2,1)}, bf16[4,512,256]{2,1,0:T(8,128)(2,1)}, u32[]{:S(2)}, u32[]{:S(2)}) collective-permute-start(bf16[4,512,256]{2,1,0:T(8,128)(2,1)} %constant_dynamic-update-slice_fusion.refs_6_), channel_id=1, source_target_pairs={{0,96},{1,97},{2,98},{3,99},{4,28},{5,29},{6,30},{7,31},{8,104},{9... | collective-permute-start | bytes 3145736 | tf_op jit(solution)/shard_map/ppermute | solution.py:62
  95.4 35.2 %collective-permute-start.15 = (bf16[4,512,256]{2,1,0:T(8,128)(2,1)S(1)}, bf16[4,512,256]{2,1,0:T(8,128)(2,1)}, u32[]{:S(2)}, u32[]{:S(2)}) collective-permute-start(bf16[4,512,256]{2,1,0:T(8,128)(2,1)S(1)} %pad_maximum_fusion.refs_5_), channel_id=1, source_target_pairs={{0,96},{1,97},{2,98},{3,99},{4,28},{5,29},{6,30},{7,31},{8,104},{9... | collective-permute-start | bytes 3145736 | tf_op jit(solution)/shard_map/ppermute | solution.py:62
  96.2 34.4 %collective-permute-start.14 = (bf16[4,512,256]{2,1,0:T(8,128)(2,1)}, bf16[4,512,256]{2,1,0:T(8,128)(2,1)}, u32[]{:S(2)}, u32[]{:S(2)}) collective-permute-start(bf16[4,512,256]{2,1,0:T(8,128)(2,1)} %constant_dynamic-update-slice_fusion.refs_6_), channel_id=1, source_target_pairs={{0,32},{1,33},{2,34},{3,35},{4,12},{5,13},{6,14},{7,15},{8,40},{9,... | collective-permute-start | bytes 3145736 | tf_op jit(solution)/shard_map/ppermute | solution.py:62
  97.6 48.2 %collective-permute-start.8 = (bf16[4,512,256]{2,1,0:T(8,128)(2,1)}, bf16[4,512,256]{2,1,0:T(8,128)(2,1)}, u32[]{:S(2)}, u32[]{:S(2)}) collective-permute-start(bf16[4,512,256]{2,1,0:T(8,128)(2,1)} %collective-permute-done.7.refs_5_), channel_id=1, source_target_pairs={{0,32},{1,33},{2,34},{3,35},{4,12},{5,13},{6,14},{7,15},{8,40},{9,... | collective-permute-start | bytes 3145736 | tf_op jit(solution)/shard_map/ppermute | solution.py:62
  97.7 48.1 %collective-permute-start.13 = (bf16[4,512,256]{2,1,0:T(8,128)(2,1)}, bf16[4,512,256]{2,1,0:T(8,128)(2,1)}, u32[]{:S(2)}, u32[]{:S(2)}) collective-permute-start(bf16[4,512,256]{2,1,0:T(8,128)(2,1)} %collective-permute-done.12.refs_8_), channel_id=1, source_target_pairs={{0,96},{1,97},{2,98},{3,99},{4,28},{5,29},{6,30},{7,31},{8,104},{9... | collective-permute-start | bytes 3145736 | tf_op jit(solution)/shard_map/ppermute | solution.py:62
  115.3 3.2 %collective-permute-start.4 = (bf16[512,512]{1,0:T(8,128)(2,1)}, bf16[512,512]{1,0:T(8,128)(2,1)S(1)}, u32[]{:S(2)}, u32[]{:S(2)}) collective-permute-start(bf16[512,512]{1,0:T(8,128)(2,1)} %get-tuple-element.20), channel_id=1, source_target_pairs={{0,4},{1,5},{2,6},{3,7},{4,0},{5,1},{6,2},{7,3},{8,12},{9,13},{10,... | collective-permute-start | bytes 1572872 | tf_op jit(solution)/shard_map/ppermute | solution.py:62
  118.5 41.6 %slice-start = ((s8[8388608]{0:T(1024)(128)(4,1)}), s8[4194304]{0:T(1024)(128)(4,1)S(1)}, s32[]{:S(2)}) async-start(s8[8388608]{0:T(1024)(128)(4,1)} %bitcast.29), calls=%async_computation | async-start | bytes 8388608
  158.0 2.1 %collective-permute-start.16 = (bf16[512,512]{1,0:T(8,128)(2,1)S(1)}, bf16[512,512]{1,0:T(8,128)(2,1)S(1)}, u32[]{:S(2)}, u32[]{:S(2)}) collective-permute-start(bf16[512,512]{1,0:T(8,128)(2,1)S(1)} %get-tuple-element.24), channel_id=1, source_target_pairs={{0,4},{1,5},{2,6},{3,7},{4,0},{5,1},{6,2},{7,3},{8,12},{9,13},{10,... | collective-permute-start | bytes 1572872 | tf_op jit(solution)/shard_map/ppermute | solution.py:62
  161.7 16.2 %collective-permute-start.17 = (bf16[128,2048]{1,0:T(8,128)(2,1)S(1)}, bf16[128,2048]{1,0:T(8,128)(2,1)S(1)}, u32[]{:S(2)}, u32[]{:S(2)}) collective-permute-start(bf16[128,2048]{1,0:T(8,128)(2,1)S(1)} %get-tuple-element.25), channel_id=1, source_target_pairs={{0,1},{1,2},{2,3},{3,0},{4,5},{5,6},{6,7},{7,4},{8,9},{9,10},{10,1... | collective-permute-start | bytes 1572872 | tf_op jit(solution)/shard_map/ppermute | solution.py:62
  162.3 15.9 %collective-permute-start.20 = (bf16[128,2048]{1,0:T(8,128)(2,1)S(1)}, bf16[128,2048]{1,0:T(8,128)(2,1)S(1)}, u32[]{:S(2)}, u32[]{:S(2)}) collective-permute-start(bf16[128,2048]{1,0:T(8,128)(2,1)S(1)} %get-tuple-element.29), channel_id=1, source_target_pairs={{0,3},{1,0},{2,1},{3,2},{4,7},{5,4},{6,5},{7,6},{8,11},{9,8},{10,9... | collective-permute-start | bytes 1572872 | tf_op jit(solution)/shard_map/ppermute | solution.py:62
  178.1 14.9 %collective-permute-start.18 = (bf16[128,2048]{1,0:T(8,128)(2,1)S(1)}, bf16[128,2048]{1,0:T(8,128)(2,1)S(1)}, u32[]{:S(2)}, u32[]{:S(2)}) collective-permute-start(bf16[128,2048]{1,0:T(8,128)(2,1)S(1)} %add_convert_fusion.3), channel_id=1, source_target_pairs={{0,1},{1,2},{2,3},{3,0},{4,5},{5,6},{6,7},{7,4},{8,9},{9,10},{10,1... | collective-permute-start | bytes 1572872 | tf_op jit(solution)/shard_map/ppermute | solution.py:62
  178.3 14.9 %collective-permute-start.21 = (bf16[128,2048]{1,0:T(8,128)(2,1)S(1)}, bf16[128,2048]{1,0:T(8,128)(2,1)S(1)}, u32[]{:S(2)}, u32[]{:S(2)}) collective-permute-start(bf16[128,2048]{1,0:T(8,128)(2,1)S(1)} %add_convert_fusion.1), channel_id=1, source_target_pairs={{0,3},{1,0},{2,1},{3,2},{4,7},{5,4},{6,5},{7,6},{8,11},{9,8},{10,9... | collective-permute-start | bytes 1572872 | tf_op jit(solution)/shard_map/ppermute | solution.py:62
  193.1 14.0 %collective-permute-start.19 = (bf16[128,2048]{1,0:T(8,128)(2,1)S(1)}, bf16[128,2048]{1,0:T(8,128)(2,1)S(1)}, u32[]{:S(2)}, u32[]{:S(2)}) collective-permute-start(bf16[128,2048]{1,0:T(8,128)(2,1)S(1)} %add_convert_fusion.2), channel_id=1, source_target_pairs={{0,1},{1,2},{2,3},{3,0},{4,5},{5,6},{6,7},{7,4},{8,9},{9,10},{10,1... | collective-permute-start | bytes 1572872 | tf_op jit(solution)/shard_map/ppermute | solution.py:62
  193.3 13.9 %collective-permute-start.22 = (bf16[128,2048]{1,0:T(8,128)(2,1)S(1)}, bf16[128,2048]{1,0:T(8,128)(2,1)S(1)}, u32[]{:S(2)}, u32[]{:S(2)}) collective-permute-start(bf16[128,2048]{1,0:T(8,128)(2,1)S(1)} %add_convert_fusion), channel_id=1, source_target_pairs={{0,3},{1,0},{2,1},{3,2},{4,7},{5,4},{6,5},{7,6},{8,11},{9,8},{10,9... | collective-permute-start | bytes 1572872 | tf_op jit(solution)/shard_map/ppermute | solution.py:62
  (16 other events, 138.8 us)

commit v2 on v1

v2 whole, which is shorter than its diff:
```python
import functools

import jax
import jax.numpy as jnp
from jax import lax
from jax.experimental import pallas as pl
from jax.experimental.pallas import tpu as pltpu
from jax.sharding import PartitionSpec as P


HEAD_DIM = 128
NY, NX, NZ = 4, 4, 4
GROUPS = 32
TOK = 128
ROWS = NZ * TOK
TILE = 16
SPAN_BITS = 9
TILES = ROWS // TILE
LOG2E = 1.4426950408889634

rope_base = 500000.0
norm_eps = 1e-05
score_floor = -1e30

AXES = ("dp", "tp")
VMEM = pltpu.VMEM


def group_of(y, x, core):
    return ((y % NY) * NX + (x % NX)) * 2 + core


def pairs(move):
    out = []
    for y in range(NY):
        for x in range(NX):
            for core in range(2):
                for z in range(NZ):
                    y2, x2, core2, z2 = move(y, x, core, z)
                    out.append(
                        (group_of(y, x, core) * NZ + z, group_of(y2, x2, core2) * NZ + z2 % NZ)
                    )
    return out


def first_axis(s):
    return pairs(
        lambda y, x, core, z: (y, x + s, core, z) if core == 0 else (y + s, x, core, z)
    )


def second_axis(s):
    return pairs(
        lambda y, x, core, z: (y + s, x, core, z) if core == 0 else (y, x + s, core, z)
    )


def along_z(s):
    return pairs(lambda y, x, core, z: (y, x, core, z + s))


def send(array, moves):
    return lax.ppermute(array, AXES, moves)


def swap_cores(array):
    return send(array, pairs(lambda y, x, core, z: (y, x, 1 - core, z)))


def cost(flops, nbytes, exps=0):
    return pl.CostEstimate(flops=int(flops), bytes_accessed=int(nbytes), transcendentals=int(exps))


def whole():
    return pl.BlockSpec(memory_space=VMEM)


def scalars():
    return pl.BlockSpec(memory_space=pltpu.SMEM)


def small():
    return pltpu.CompilerParams(vmem_limit_bytes=8 * 2**20)


def norm_kernel(tokens_ref, gain_ref, low_ref, high_ref):
    gain = gain_ref[...]
    half = low_ref.shape[0]

    for first, out_ref in ((0, low_ref), (half, high_ref)):

        def chunk(i, _):
            at = pl.multiple_of(i * 16, 16)
            rows = tokens_ref[pl.ds(first + at, 16), :].astype(jnp.float32)
            scale = lax.rsqrt(jnp.mean(rows * rows, axis=1, keepdims=True) + norm_eps)
            out_ref[pl.ds(at, 16), :] = (rows * scale * gain).astype(jnp.bfloat16)
            return 0

        lax.fori_loop(0, half // 16, chunk, 0)


def normalise(tokens, gain):
    rows, width = tokens.shape
    return pl.pallas_call(
        norm_kernel,
        out_shape=[jax.ShapeDtypeStruct((rows // 2, width), jnp.bfloat16)] * 2,
        in_specs=[whole(), whole()],
        out_specs=[whole(), whole()],
        compiler_params=small(),
        cost_estimate=cost(rows * width * 5, rows * width * 4),
    )(tokens, gain.reshape(1, width))


def as_column(row):
    return jnp.broadcast_to(row, (128, 128)).T


def order_kernel(packed_ref, out_ref):
    lane = lax.broadcasted_iota(jnp.int32, (128, 128), 1).astype(jnp.float32)
    blocks = ROWS // 128

    def one_group(g, _):
        row = packed_ref[pl.ds(g, 1), :]
        pieces = [row[:, i * 128 : (i + 1) * 128] for i in range(blocks)]
        sums = [jnp.zeros((128, 128), jnp.float32) for _ in range(blocks)]
        for j in range(blocks):
            column = as_column(pieces[j])
            below = jnp.zeros((128, 128), jnp.float32)
            for i in range(blocks):
                below = below + jnp.where(pieces[i] < column, 1.0, 0.0)
            rank = jnp.sum(below, axis=1, keepdims=True)
            for i in range(blocks):
                sums[i] = sums[i] + jnp.where(rank == lane + float(i * 128), column, 0.0)
        out_ref[pl.ds(g, 1), :] = jnp.concatenate(
            [jnp.sum(s, axis=0, keepdims=True) for s in sums], axis=1
        )
        return 0

    lax.fori_loop(0, GROUPS, one_group, 0)


def order_groups(packed):
    return pl.pallas_call(
        order_kernel,
        out_shape=jax.ShapeDtypeStruct((GROUPS, ROWS), jnp.float32),
        in_specs=[whole()],
        out_specs=whole(),
        compiler_params=small(),
        cost_estimate=cost(6 * GROUPS * ROWS * ROWS, 8 * GROUPS * ROWS),
    )(packed)


def column_kernel(packed_ref, out_ref):
    def one(u, _):
        at = pl.ds(pl.multiple_of(u * 128, 128), 128)
        out_ref[at, :] = as_column(packed_ref[pl.ds(u, 1), :])
        return 0

    lax.fori_loop(0, TILES, one, 0)


def columns_of(packed):
    return pl.pallas_call(
        column_kernel,
        out_shape=jax.ShapeDtypeStruct((TILES * 128, 128), jnp.int32),
        in_specs=[whole()],
        out_specs=whole(),
        compiler_params=small(),
        cost_estimate=cost(TILES * 128 * 128 * 32, TILES * 128 * 512),
    )(packed)


def turn(head, cosine, sine):
    return head * cosine + pltpu.roll(head, HEAD_DIM // 2, 1) * sine


def stacked(refs):
    if len(refs) == 1:
        return refs[0][...]
    return jnp.concatenate([ref[...] for ref in refs], axis=0)


def keys_and_values(rows, wk_ref, wv_ref, cosine, sine):
    keys = jnp.dot(rows, wk_ref[...], preferred_element_type=jnp.float32)
    values = jnp.dot(rows, wv_ref[...], preferred_element_type=jnp.float32)
    out = []
    for head in range(2):
        at = slice(head * HEAD_DIM, (head + 1) * HEAD_DIM)
        key = turn(keys[:, at], cosine, sine)
        out.append(jnp.concatenate([key, values[:, at]], axis=1).astype(jnp.bfloat16))
    return out


def kv_kernel(parts, first, *refs):
    wk_ref, wv_ref, cos_ref, sin_ref, out_ref = refs[parts:]
    rows = stacked(refs[:parts])
    at = slice(first, first + rows.shape[0])
    for head, block in enumerate(
        keys_and_values(rows, wk_ref, wv_ref, cos_ref[at, :], sin_ref[at, :])
    ):
        out_ref[head] = block


def project_kv(pieces, w_key, w_value, cosine, sine, first):
    width = w_key.shape[0]
    rows = sum(p.shape[0] for p in pieces)
    return pl.pallas_call(
        functools.partial(kv_kernel, len(pieces), first),
        out_shape=jax.ShapeDtypeStruct((2, rows, 256), jnp.bfloat16),
        in_specs=[whole()] * (len(pieces) + 4),
        out_specs=whole(),
        compiler_params=small(),
        cost_estimate=cost(2 * rows * width * 512, width * 1024 + rows * width * 2),
    )(*pieces, w_key, w_value, cosine, sine)


def sorting(rank_row):
    slot = lax.broadcasted_iota(jnp.int32, (ROWS, ROWS), 0)
    return (slot == rank_row).astype(jnp.bfloat16)


def last_kv_kernel(parts, core_ref, *refs):
    wk_ref, wv_ref, cos_ref, sin_ref, rank_ref = refs[parts : parts + 5]
    done_refs, (other_ref, mine_ref) = refs[parts + 5 : -3], refs[-3:-1]
    last_ref = refs[-1]
    rows = stacked(refs[:parts])
    at = slice(ROWS - rows.shape[0], ROWS)
    for head, block in enumerate(
        keys_and_values(rows, wk_ref, wv_ref, cos_ref[at, :], sin_ref[at, :])
    ):
        last_ref[head] = block
    pick = sorting(rank_ref[...])
    core = core_ref[0]
    for head, out_ref in ((1 - core, other_ref), (core, mine_ref)):
        rows = jnp.concatenate([ref[head] for ref in (*done_refs, last_ref)], axis=0)
        out_ref[...] = jnp.dot(pick, rows, preferred_element_type=jnp.float32).astype(jnp.bfloat16)


def finish_kv(core, pieces, w_key, w_value, cosine, sine, rank_row, done):
    width = w_key.shape[0]
    rows = sum(p.shape[0] for p in pieces)
    shape = jax.ShapeDtypeStruct((ROWS, 256), jnp.bfloat16)
    return pl.pallas_call(
        functools.partial(last_kv_kernel, len(pieces)),
        out_shape=(shape, shape),
        in_specs=[scalars()] + [whole()] * (len(pieces) + 5 + len(done)),
        out_specs=(whole(), whole()),
        scratch_shapes=[pltpu.VMEM((2, rows, 256), jnp.bfloat16)],
        compiler_params=small(),
        cost_estimate=cost(2 * rows * width * 512, width * 1024 + rows * width * 2),
    )(core, *pieces, w_key, w_value, cosine, sine, rank_row, *done)


def q_kernel(parts, mine, core_ref, *refs):
    w_ref, cos_ref, sin_ref, rank_ref, out_ref, turned_ref = refs[parts:]
    half = core_ref[0] if mine else 1 - core_ref[0]
    for block in range(NZ):
        rows = stacked(refs[2 * block : 2 * block + 2])
        at = slice(block * TOK, (block + 1) * TOK)
        cosine, sine = cos_ref[at, :], sin_ref[at, :]
        for first in range(0, 512, 256):
            columns = pl.ds(pl.multiple_of(half * 512 + first, 256), 256)
            both = jnp.dot(rows, w_ref[:, columns], preferred_element_type=jnp.float32)
            turned = jnp.concatenate(
                [turn(both[:, :HEAD_DIM], cosine, sine), turn(both[:, HEAD_DIM:], cosine, sine)],
                axis=1,
            )
            turned_ref[at, first : first + 256] = (
                turned * (HEAD_DIM ** (-0.5) * LOG2E)
            ).astype(jnp.bfloat16)
    out_ref[...] = jnp.dot(
        sorting(rank_ref[...]), turned_ref[...], preferred_element_type=jnp.float32
    ).astype(jnp.bfloat16)


def project_q(core, pieces, w_query, cosine, sine, rank_row, mine):
    width = w_query.shape[0]
    return pl.pallas_call(
        functools.partial(q_kernel, len(pieces), mine),
        out_shape=jax.ShapeDtypeStruct((ROWS, 512), jnp.bfloat16),
        in_specs=[scalars()] + [whole()] * (len(pieces) + 4),
        out_specs=whole(),
        scratch_shapes=[pltpu.VMEM((ROWS, 512), jnp.bfloat16)],
        compiler_params=small(),
        cost_estimate=cost(2 * ROWS * width * 512, width * 1024 + ROWS * width * 2),
    )(core, *pieces, w_query, cosine, sine, rank_row)


def attend_kernel(opening, closing, batch, count, low_ref, high_ref, *refs):
    q_refs, refs = refs[:2], refs[2:]
    key_at_ref, bound_ref = refs[:2]
    kv_refs, refs = refs[2 : 2 + count], refs[2 + count :]
    if not opening:
        old_ref, refs = refs[0], refs[1:]
    if closing:
        w_from, out_refs, (w_to, state_ref, arrived) = refs[0], refs[1:3], refs[3:]
        copy = pltpu.make_async_copy(w_from, w_to, arrived)
        copy.start()
    else:
        (state_ref,) = refs

    def at(u, size):
        return pl.ds(pl.multiple_of(u * size, size), size)

    def queries(u):
        return jnp.concatenate(
            [
                ref[at(u, TILE), h * HEAD_DIM : (h + 1) * HEAD_DIM]
                for ref in q_refs
                for h in range(4)
            ],
            axis=0,
        )

    def keys(t):
        return jnp.concatenate(
            [ref[:, at(t, TILE), :].reshape(-1, 256) for ref in kv_refs], axis=0
        )

    def spread(a, wide=1):
        a = jnp.broadcast_to(a, (128, 128))
        return a if wide == 1 else jnp.concatenate([a] * wide, axis=1)

    def update(us, kvs, key_ats, states):
        wide = kvs[0].shape[0] // 128
        scores = [
            lax.dot_general(
                queries(u),
                kv[:, :HEAD_DIM],
                (((1,), (1,)), ((), ())),
                preferred_element_type=jnp.float32,
            )
            for u, kv in zip(us, kvs)
        ]
        masked = []
        for u, score, key_at in zip(us, scores, key_ats):
            bound = bound_ref[at(u, 128), :]
            upper = bound >> SPAN_BITS
            lower = upper - (bound & (2**SPAN_BITS - 1))
            allowed = (key_at <= spread(upper, wide)) & (key_at >= spread(lower, wide))
            masked.append(jnp.where(allowed, score, score_floor))
        peaks = [spread(jnp.max(m, axis=1, keepdims=True)) for m in masked]
        peaks = [p if st is None else jnp.maximum(p, st[0]) for p, st in zip(peaks, states)]
        weights = [jnp.exp2(m - spread(p, wide)) for m, p in zip(masked, peaks)]
        totals = [spread(jnp.sum(w, axis=1, keepdims=True)) for w in weights]
        mixes = [
            jnp.dot(w.astype(jnp.bfloat16), kv[:, HEAD_DIM:], preferred_element_type=jnp.float32)
            for w, kv in zip(weights, kvs)
        ]
        out = []
        for peak, total, mixed, st in zip(peaks, totals, mixes, states):
            if st is not None:
                keep = jnp.exp2(st[0] - peak)
                total = total + st[1] * keep
                mixed = mixed + st[2] * keep
            out.append((peak, total, mixed))
        return out

    def load(ref, u):
        return tuple(ref[at(u, 128), i * 128 : (i + 1) * 128] for i in range(3))

    def save(u, state):
        for i, part in enumerate(state):
            state_ref[at(u, 128), i * 128 : (i + 1) * 128] = part

    def write(u, state):
        _, total, mixed = state
        context = (mixed / total).astype(jnp.bfloat16)
        for i, ref in enumerate(out_refs):
            for h in range(4):
                block = (i * 4 + h) * TILE
                ref[at(u, TILE), h * HEAD_DIM : (h + 1) * HEAD_DIM] = context[block : block + TILE]

    def finish(us, states):
        for u, state in zip(us, states):
            save(u, state)
            if closing:
                write(u, state)

    def some(i, _):
        us = [batch * i + n for n in range(batch)]
        kvs, key_ats = [], []
        for u in us:
            low, high = low_ref[u], high_ref[u]
            t0 = jnp.minimum(low, TILES - 1)
            t1 = jnp.minimum(low + 1, TILES - 1)
            at0 = jnp.where(low < high, key_at_ref[pl.ds(t0, 1), :], -1)
            at1 = jnp.where(low + 1 < high, key_at_ref[pl.ds(t1, 1), :], -1)
            kvs.append(jnp.concatenate([keys(t0), keys(t1)], axis=0))
            key_ats.append(jnp.concatenate([at0, at1], axis=1))
        states = [None if opening else load(old_ref, u) for u in us]
        finish(us, update(us, kvs, key_ats, states))
        return 0

    lax.fori_loop(0, TILES // batch, some, 0)

    def rest(u, _):
        def more(t, _):
            key_at = key_at_ref[pl.ds(t, 1), :]
            finish([u], update([u], [keys(t)], [key_at], [load(state_ref, u)]))
            return 0

        return lax.fori_loop(low_ref[u] + 2, high_ref[u], more, 0)

    lax.fori_loop(0, TILES, rest, 0)
    if closing:
        copy.wait()


def attend(bounds, queries, key_at, row_bounds, kvs, state, batch, resident=None):
    opening, closing = state is None, resident is not None
    running = jax.ShapeDtypeStruct((TILES * 128, 384), jnp.float32)
    operands = [*bounds, *queries, key_at, row_bounds, *kvs, *(() if opening else (state,))]
    in_specs = [scalars(), scalars()] + [whole()] * (len(operands) - 2)
    out_shape, out_specs, scratch = running, whole(), ()
    if closing:
        operands.append(resident)
        in_specs.append(pl.BlockSpec(memory_space=pltpu.HBM))
        context = jax.ShapeDtypeStruct((ROWS, 512), jnp.bfloat16)
        out_shape = [context, context, jax.ShapeDtypeStruct(resident.shape, resident.dtype)]
        out_specs = [whole()] * 3
        scratch = [pltpu.VMEM((TILES * 128, 384), jnp.float32), pltpu.SemaphoreType.DMA]
    rows = sum(kv.shape[0] for kv in kvs) * TILE * 2
    return pl.pallas_call(
        functools.partial(attend_kernel, opening, closing, batch, len(kvs)),
        out_shape=out_shape,
        in_specs=in_specs,
        out_specs=out_specs,
        scratch_shapes=scratch,
        compiler_params=pltpu.CompilerParams(vmem_limit_bytes=(29 if closing else 8) * 2**20),
        cost_estimate=cost(TILES * 128 * rows * 512, 10e6, TILES * 128 * rows),
    )(*operands)


def unsort(rank_row, block, parts):
    slot = lax.broadcasted_iota(jnp.int32, (TOK, ROWS), 1)
    rank = as_column(rank_row[:, block * TOK : (block + 1) * TOK])
    pick = (slot == jnp.concatenate([rank] * (ROWS // 128), axis=1)).astype(jnp.bfloat16)
    return [
        jnp.dot(pick, part[...], preferred_element_type=jnp.float32).astype(jnp.bfloat16)
        for part in parts
    ]


def product_kernel(wanted, core_ref, rank_ref, mine_ref, other_ref, w_ref, *out_refs):
    core = core_ref[0]
    mine_at = pl.ds(pl.multiple_of(core * 512, 512), 512)
    other_at = pl.ds(pl.multiple_of((1 - core) * 512, 512), 512)
    part = w_ref.shape[1] // 4
    rank = rank_ref[...]
    rows = {}
    for block, _ in wanted:
        if block not in rows:
            rows[block] = unsort(rank, block, (mine_ref, other_ref))
    for side in range(4):
        group = [(i, block) for i, (block, s) in enumerate(wanted) if s == side]
        mine = jnp.concatenate([rows[block][0] for _, block in group], axis=0)
        other = jnp.concatenate([rows[block][1] for _, block in group], axis=0)
        at = slice(side * part, (side + 1) * part)
        product = jnp.dot(
            mine, w_ref[mine_at, at], preferred_element_type=jnp.float32
        ) + jnp.dot(other, w_ref[other_at, at], preferred_element_type=jnp.float32)
        for n, (i, _) in enumerate(group):
            out_refs[i][...] = product[n * TOK : (n + 1) * TOK].astype(jnp.bfloat16)


def products(core, rank_row, mine, other, w_output, wanted):
    width = w_output.shape[1]
    shape = jax.ShapeDtypeStruct((TOK, width // 4), jnp.bfloat16)
    return pl.pallas_call(
        functools.partial(product_kernel, wanted),
        out_shape=[shape] * len(wanted),
        in_specs=[scalars()] + [whole()] * 4,
        out_specs=[whole()] * len(wanted),
        compiler_params=small(),
        cost_estimate=cost(TOK * 512 * width * len(wanted), 1024 * width * 2),
    )(core, rank_row, mine, other, w_output)


def document_start(position, starts):
    reached = starts <= position[..., None]
    return jnp.max(jnp.where(reached, starts, 0), axis=-1)


def layer(tokens, norm_gain, w_query, w_key, w_value, w_output, doc_lengths, pack_index):
    group = lax.axis_index("dp")
    z = lax.axis_index("tp")
    core = group % 2
    chip_x = (group // 2) % NX
    chip_y = group // (2 * NX)
    core_arg = core.astype(jnp.int32).reshape(1)

    own_low, own_high = normalise(tokens, norm_gain)
    below_low = send(own_low, along_z(1))
    above_high = send(own_high, along_z(-1))
    below_high = send(own_high, along_z(1))
    above_low = send(own_low, along_z(-1))
    far_low = send(below_low, along_z(1))
    far_high = send(above_high, along_z(-1))
    own_rows = (own_low, own_high)
    near_rows = (below_low, below_high, above_low, above_high)
    far_rows = (far_low, far_high)

    number = jnp.arange(doc_lengths.shape[0], dtype=jnp.int32)
    starts = jnp.sum(jnp.where(number[None, :] < number[:, None], doc_lengths[None, :], 0), axis=1)
    by_group = pack_index.reshape(GROUPS, NZ, TOK)
    own = lax.dynamic_index_in_dim(by_group, group, 0, keepdims=False)
    order = (z + jnp.array([0, NZ - 1, 1, 2], jnp.int32)) % NZ
    packed = jnp.take(own, order, axis=0).reshape(ROWS)
    place = packed - document_start(packed, starts)
    rank_row = jnp.sum((packed[:, None] < packed[None, :]).astype(jnp.int32), axis=0)
    rank_row = rank_row.reshape(1, ROWS)
    half_dim = HEAD_DIM // 2
    frequency = rope_base ** (-2.0 * jnp.arange(half_dim, dtype=jnp.float32) / HEAD_DIM)
    angles = place.astype(jnp.float32)[:, None] * frequency[None, :]
    cosine, sine = jnp.cos(angles), jnp.sin(angles)
    cosine = jnp.concatenate([cosine, cosine], axis=1)
    sine = jnp.concatenate([-sine, sine], axis=1)

    kv_own = project_kv(own_rows, w_key, w_value, cosine, sine, 0)

    ordered = order_groups(pack_index.reshape(GROUPS, ROWS).astype(jnp.float32))
    ordered = ordered.astype(jnp.int32)
    offsets = jnp.array([0, -1, 1, 2], jnp.int32)
    outer, inner = offsets[:, None, None], offsets[None, :, None]
    which = (core + jnp.arange(2, dtype=jnp.int32)) % 2
    dy = jnp.where(core == 0, outer, inner)
    dx = jnp.where(core == 0, inner, outer)
    source = (((chip_y + dy) % NY) * NX + (chip_x + dx) % NX) * 2 + which[None, None, :]
    key_at = jnp.take(ordered, source.reshape(GROUPS), axis=0)
    key_at = key_at.reshape(GROUPS, TILES, TILE).transpose(1, 0, 2)
    rows_at = jnp.take(ordered, jnp.stack([group, group + 1 - 2 * core]), axis=0)
    rows_from = document_start(rows_at, starts)
    rows_at = rows_at.reshape(2, TILES, TILE)
    rows_from = rows_from.reshape(2, TILES, TILE)
    first_needed = jnp.min(rows_from, axis=(0, 2))
    last_needed = jnp.max(rows_at, axis=(0, 2))

    def per_row(a):
        a = jnp.broadcast_to(a.transpose(1, 0, 2)[:, :, None, :], (TILES, 2, 4, TILE))
        return a.reshape(TILES, 128)

    row_bounds = columns_of(per_row(rows_at * 2**SPAN_BITS + rows_at - rows_from))
    key_parts, windows = [], []
    for first, count in ((0, 24), (24, 8)):
        part = key_at[:, first : first + count].reshape(TILES, count * TILE)
        tile_first = jnp.min(part, axis=1)
        tile_last = jnp.max(part, axis=1)
        low = jnp.sum((tile_last[None, :] < first_needed[:, None]).astype(jnp.int32), axis=1)
        high = jnp.sum((tile_first[None, :] <= last_needed[:, None]).astype(jnp.int32), axis=1)
        key_parts.append(part)
        windows.append((low, high))
    cosine, sine, row_bounds, key_parts, windows = lax.optimization_barrier(
        (cosine, sine, row_bounds, key_parts, windows)
    )

    kv_near = project_kv(near_rows, w_key, w_value, cosine, sine, TOK)
    kv_other, kv_mine = finish_kv(
        core_arg, far_rows, w_key, w_value, cosine, sine, rank_row, (kv_own, kv_near)
    )
    kv_partner = swap_cores(kv_other)
    chip = jnp.concatenate([kv_mine[None], kv_partner[None]], axis=0)

    back = send(chip, first_axis(1))
    ahead = send(chip, first_axis(-1))
    chip_b = send(chip, second_axis(1))
    chip_a = send(chip, second_axis(-1))
    far = send(ahead, first_axis(-1))
    back_b = send(back, second_axis(1))
    ahead_a = send(ahead, second_axis(-1))
    ahead_b = send(ahead, second_axis(1))
    back_a = send(back, second_axis(-1))
    end_b = send(far, second_axis(1))
    end_a = send(far, second_axis(-1))
    chip_f = send(chip_b, second_axis(1))
    back_f = send(back_b, second_axis(1))
    ahead_f = send(ahead_a, second_axis(-1))
    end_f = send(end_a, second_axis(-1))

    pieces = (*own_rows, *near_rows, *far_rows)
    q_other = project_q(core_arg, pieces, w_query, cosine, sine, rank_row, False)
    q_mine = project_q(core_arg, pieces, w_query, cosine, sine, rank_row, True)
    q_partner = swap_cores(q_other)
    queries = (q_mine, q_partner)

    near_kv = (chip, back, ahead, far)
    near_kv += (chip_b, back_b, ahead_b, end_b, chip_a, back_a, ahead_a, end_a)
    state = attend(
        windows[0], queries, key_parts[0], row_bounds, near_kv, None, 4
    )
    state = attend(
        windows[1],
        queries,
        key_parts[1],
        row_bounds,
        (chip_f, back_f, ahead_f, end_f),
        state,
        8,
        w_output,
    )
    mine, partner, w_near = state
    other = swap_cores(partner)

    def plus(a, b):
        return a.astype(jnp.float32) + b.astype(jnp.float32)

    ways = (along_z(1), along_z(1), along_z(-1), along_z(-1))
    moving = products(
        core_arg, rank_row, mine, other, w_near, ((1, 0), (1, 1), (2, 2), (2, 3))
    )
    moving = [send(a, way) for a, way in zip(moving, ways)]
    terms = products(
        core_arg,
        rank_row,
        mine,
        other,
        w_near,
        tuple(
            (block, side)
            for blocks in ((3, 3, 3, 3), (2, 2, 1, 1), (0, 0, 0, 0))
            for side, block in enumerate(blocks)
        ),
    )
    for first in (0, 4):
        moving = [
            send(plus(a, b).astype(jnp.bfloat16), way)
            for a, b, way in zip(moving, terms[first : first + 4], ways)
        ]
    attended = jnp.concatenate([plus(a, b) for a, b in zip(moving, terms[8:])], axis=1)
    return (tokens.astype(jnp.float32) + attended).astype(jnp.bfloat16)


def solution(mesh):
    placed = (
        P(("dp", "tp"), None),
        P(),
        P(None, "tp"),
        P(None, "tp"),
        P(None, "tp"),
        P("tp", None),
        P(),
        P(),
    )
    return jax.shard_map(
        layer, mesh=mesh, in_specs=placed, out_specs=P(("dp", "tp"), None), check_vma=False
    )
```

time: 210 us -> 171 us (0.81)
  waiting for transfers between devices: 71.5 us -> 38.6 us
  Pallas kernels: 75.7 us -> 53.4 us
  starting transfers between devices: 36 us -> 51.4 us
  other arithmetic: 7.34 us -> 12.6 us
  local copies, waits for them, and re-layouts: 18.5 us -> 13.5 us
    ppermute x23 -> x36, waiting for transfers between devices: 71.5 us -> 38.6 us  [send(): return lax.ppermute(array, AXES, moves)]
    pallas_call x5 -> x6, Pallas kernels: 51.5 us -> 29.9 us  [the longest x2 14.7 us: attend(): pl.pallas_call(functools.partial(attend_kernel, opening, closing, batch,...]
    ppermute x23 -> x36, starting transfers between devices: 36 us -> 51.4 us  [send(): return lax.ppermute(array, AXES, moves)]
    slice x4 -> x0, local copies, waits for them, and re-layouts: 3.8 us -> none  [the longest x1 1.89 us: layer(): far_low = send(below[:TOK // 2], along_z(1))]
    unnamed x36 -> x34, local copies, waits for them, and re-layouts: 10.6 us -> 9.09 us
  transfers between devices with their start and end apart: 23 -> 36, of which waited for: 10 -> 13; matrix products, arithmetic and copies ran while one was open for 7% -> 9% of each run, Pallas kernels for 27% -> 25%
where the time goes in v2:
time: 171 us; the launch traced here: 170 us
  Pallas kernels  53.4 us (31%)
  starting transfers between devices  51.4 us (30%)
  waiting for transfers between devices  38.6 us (23%)
  local copies, waits for them, and re-layouts  13.5 us (8%)
  other arithmetic  12.6 us (7%)
    ppermute x36, starting transfers between devices, send(): return lax.ppermute(array, AXES, moves)  51.4 us
    ppermute x36, waiting for transfers between devices, send(): return lax.ppermute(array, AXES, moves)  38.6 us
    pallas_call x2, Pallas kernels, attend(): pl.pallas_call(functools.partial(attend_kernel, opening, closing, batch,...  14.7 us
    pallas_call x1, Pallas kernels, order_groups(): pl.pallas_call(order_kernel, out_shape=jax.ShapeDtypeStruct((GROUPS, ROWS...  10.6 us
    pallas_call x2, Pallas kernels, project_q(): pl.pallas_call(functools.partial(q_kernel, len(pieces), mine), out_shape=...  10 us
    unnamed x34, local copies, waits for them, and re-layouts  9.09 us
    pallas_call x2, Pallas kernels, products(): pl.pallas_call(functools.partial(product_kernel, wanted), out_shape=[shap...  5.61 us
    pallas_call x2, Pallas kernels, project_kv(): pl.pallas_call(functools.partial(kv_kernel, len(pieces), first), out_shap...  5.03 us
  transfers between devices with their start and end apart: 36, of which 13 were waited for; matrix products, arithmetic and copies ran while one was open for 9% of the time, Pallas kernels for 25%

profile of v2, /device:TPU:0, one launch (start us, length us, event | category | flops | bytes accessed | tf_op | source)
XLA Modules:
  0.0 170.1 jit_solution(5412608838103758961)
XLA Ops:
  3.9 4.1 %collective-permute-start.2 = (bf16[64,4096]{1,0:T(8,128)(2,1)S(1)}, bf16[64,4096]{1,0:T(8,128)(2,1)}, u32[]{:S(2)}, u32[]{:S(2)}) collective-permute-start(bf16[64,4096]{1,0:T(8,128)(2,1)S(1)} %get-tuple-element.39.refs_0_), channel_id=1, source_target_pairs={{0,3},{1,0},{2,1},{3,2},{4,7},{5,4},{6,5},{7,6},{8,11},{9,8},{10,9... | collective-permute-start | bytes 1572872 | tf_op jit(solution)/shard_map/ppermute | solution.py:63
  8.1 3.2 %collective-permute-start.3 = (bf16[64,4096]{1,0:T(8,128)(2,1)}, bf16[64,4096]{1,0:T(8,128)(2,1)}, u32[]{:S(2)}, u32[]{:S(2)}) collective-permute-start(bf16[64,4096]{1,0:T(8,128)(2,1)} %get-tuple-element.40.refs_1_), channel_id=1, source_target_pairs={{0,3},{1,0},{2,1},{3,2},{4,7},{5,4},{6,5},{7,6},{8,11},{9,8},{10,9... | collective-permute-start | bytes 1572872 | tf_op jit(solution)/shard_map/ppermute | solution.py:63
  16.4 10.6 %shard_map.100 = f32[32,512]{1,0:T(8,128)S(1)} custom-call(f32[32,512]{1,0:T(8,128)S(1)} %convert_element_type.136.packed_ref), custom_call_target="tpu_custom_call" | custom-call | flops 50331648 | bytes 131072 | tf_op jit(solution)/shard_map/pallas_call | solution.py:143
  33.5 3.3 %collective-permute-start.5 = (bf16[64,4096]{1,0:T(8,128)(2,1)}, bf16[64,4096]{1,0:T(8,128)(2,1)}, u32[]{:S(2)}, u32[]{:S(2)}) collective-permute-start(bf16[64,4096]{1,0:T(8,128)(2,1)} %collective-permute-done.3.refs_5_.refs_3_), channel_id=1, source_target_pairs={{0,3},{1,0},{2,1},{3,2},{4,7},{5,4},{6,5},{7,6},{8,11},{9,8},{10,9... | collective-permute-start | bytes 1572872 | tf_op jit(solution)/shard_map/ppermute | solution.py:63
  38.5 3.2 %shard_map.101.refs_3_ = s32[4096,128]{1,0:T(8,128)S(1)} custom-call(s32[32,128]{1,0:T(8,128)S(1)} %copy.21.packed_ref), custom_call_target="tpu_custom_call" | custom-call | flops 16777216 | bytes 2097152 | tf_op jit(solution)/shard_map/pallas_call | solution.py:163
  46.8 3.0 %shard_map.106.refs_8_ = bf16[2,256,256]{2,1,0:T(8,128)(2,1)S(1)} custom-call(bf16[64,4096]{1,0:T(8,128)(2,1)} %collective-permute-done.refs_2_.refs_0_, bf16[64,4096]{1,0:T(8,128)(2,1)} %collective-permute-done.1.refs_3_.refs_1_, bf16[64,4096]{1,0:T(8,128)(2,1)} %collective-permute-done.2.refs_4_.refs_2_, ...), custom_call_target="tpu_custom_call" | custom-call | flops 1073741824 | bytes 6291456 | tf_op jit(solution)/shard_map/pallas_call | solution.py:207
  53.8 3.0 %collective-permute-start.13 = (bf16[2,512,256]{2,1,0:T(8,128)(2,1)S(1)}, bf16[2,512,256]{2,1,0:T(8,128)(2,1)S(1)}, u32[]{:S(2)}, u32[]{:S(2)}) collective-permute-start(bf16[2,512,256]{2,1,0:T(8,128)(2,1)S(1)} %pad_maximum_fusion.refs_4_), channel_id=1, source_target_pairs={{0,24},{1,25},{2,26},{3,27},{4,100},{5,101},{6,102},{7,103},{8,0},... | collective-permute-start | bytes 1572872 | tf_op jit(solution)/shard_map/ppermute | solution.py:63
  56.9 5.0 %shard_map.104 = bf16[512,512]{1,0:T(8,128)(2,1)S(1)} custom-call(s32[1]{0:T(128)} %bitcast.core_ref, bf16[64,4096]{1,0:T(8,128)(2,1)S(1)} %get-tuple-element.39.refs_0_, bf16[64,4096]{1,0:T(8,128)(2,1)} %get-tuple-element.40.refs_1_, bf16[64,4096]{1,0:T(8,128)(2,1)} %collective-permute-done.refs_2_.refs_0_, ...), custom_call_target="tpu_custom_call" | custom-call | flops 2147483648 | bytes 8388608 | tf_op jit(solution)/shard_map/pallas_call | solution.py:278
  62.1 3.0 %collective-permute-start.21 = (bf16[2,512,256]{2,1,0:T(8,128)(2,1)S(1)}, bf16[2,512,256]{2,1,0:T(8,128)(2,1)S(1)}, u32[]{:S(2)}, u32[]{:S(2)}) collective-permute-start(bf16[2,512,256]{2,1,0:T(8,128)(2,1)S(1)} %pad_maximum_fusion.refs_4_), channel_id=1, source_target_pairs={{0,96},{1,97},{2,98},{3,99},{4,28},{5,29},{6,30},{7,31},{8,104},{9... | collective-permute-start | bytes 1572872 | tf_op jit(solution)/shard_map/ppermute | solution.py:63
  69.0 6.7 %collective-permute-done.21.refs_12_ = bf16[2,512,256]{2,1,0:T(8,128)(2,1)S(1)} collective-permute-done((bf16[2,512,256]{2,1,0:T(8,128)(2,1)S(1)}, bf16[2,512,256]{2,1,0:T(8,128)(2,1)S(1)}, u32[]{:S(2)}, u32[]{:S(2)}) %collective-permute-start.21) | collective-permute-done | bytes 524320 | tf_op jit(solution)/shard_map/ppermute | solution.py:63
  75.7 3.7 %collective-permute-start.14 = (bf16[2,512,256]{2,1,0:T(8,128)(2,1)S(1)}, bf16[2,512,256]{2,1,0:T(8,128)(2,1)}, u32[]{:S(2)}, u32[]{:S(2)}) collective-permute-start(bf16[2,512,256]{2,1,0:T(8,128)(2,1)S(1)} %collective-permute-done.13.refs_6_), channel_id=1, source_target_pairs={{0,96},{1,97},{2,98},{3,99},{4,28},{5,29},{6,30},{7,31},{8,104},{9... | collective-permute-start | bytes 1572872 | tf_op jit(solution)/shard_map/ppermute | solution.py:63
  86.7 5.1 %collective-permute-done.22.refs_13_ = bf16[2,512,256]{2,1,0:T(8,128)(2,1)S(1)} collective-permute-done((bf16[2,512,256]{2,1,0:T(8,128)(2,1)S(1)}, bf16[2,512,256]{2,1,0:T(8,128)(2,1)S(1)}, u32[]{:S(2)}, u32[]{:S(2)}) %collective-permute-start.22) | collective-permute-done | bytes 524320 | tf_op jit(solution)/shard_map/ppermute | solution.py:63
  92.5 3.7 %collective-permute-start.15 = (bf16[2,512,256]{2,1,0:T(8,128)(2,1)}, bf16[2,512,256]{2,1,0:T(8,128)(2,1)}, u32[]{:S(2)}, u32[]{:S(2)}) collective-permute-start(bf16[2,512,256]{2,1,0:T(8,128)(2,1)} %collective-permute-done.14.refs_14_), channel_id=1, source_target_pairs={{0,96},{1,97},{2,98},{3,99},{4,28},{5,29},{6,30},{7,31},{8,104},{9... | collective-permute-start | bytes 1572872 | tf_op jit(solution)/shard_map/ppermute | solution.py:63
  97.5 3.7 %collective-permute-start.18 = (bf16[2,512,256]{2,1,0:T(8,128)(2,1)}, bf16[2,512,256]{2,1,0:T(8,128)(2,1)}, u32[]{:S(2)}, u32[]{:S(2)}) collective-permute-start(bf16[2,512,256]{2,1,0:T(8,128)(2,1)} %collective-permute-done.17.refs_15_), channel_id=1, source_target_pairs={{0,96},{1,97},{2,98},{3,99},{4,28},{5,29},{6,30},{7,31},{8,104},{9... | collective-permute-start | bytes 1572872 | tf_op jit(solution)/shard_map/ppermute | solution.py:63
  101.3 3.4 %copy-done = bf16[4096,1024]{1,0:T(8,128)(2,1)S(1)} copy-done((bf16[4096,1024]{1,0:T(8,128)(2,1)S(1)}, bf16[4096,1024]{1,0:T(8,128)(2,1)}, u32[]{:S(2)}) %copy-start) | copy-done | bytes 8388632
  104.8 5.1 %shard_map.103.refs_0_ = bf16[512,512]{1,0:T(8,128)(2,1)S(1)} custom-call(s32[1]{0:T(128)} %bitcast.core_ref, bf16[64,4096]{1,0:T(8,128)(2,1)S(1)} %get-tuple-element.39.refs_0_, bf16[64,4096]{1,0:T(8,128)(2,1)} %get-tuple-element.40.refs_1_, bf16[64,4096]{1,0:T(8,128)(2,1)} %collective-permute-done.refs_2_.refs_0_, ...), custom_call_target="tpu_custom_call" | custom-call | flops 2147483648 | bytes 8388608 | tf_op jit(solution)/shard_map/pallas_call | solution.py:278
  109.9 9.6 %shard_map.108.refs_8_ = f32[4096,384]{1,0:T(8,128)S(1)} custom-call(s32[32]{0:T(128)S(1)} %get-tuple-element.47.low_ref, s32[32]{0:T(128)S(1)} %get-tuple-element.48.high_ref, bf16[512,512]{1,0:T(8,128)(2,1)S(1)} %shard_map.103.refs_0_, bf16[512,512]{1,0:T(8,128)(2,1)S(1)} %collective-permute-done.6.refs_1_, s32[32,384]{1,0:T(8,128)S(1)} %copy.25.refs_2_, ...), custom_call_target="tpu_custom_call" | custom-call | flops 1610612736 | bytes 10000000 | tf_op jit(solution)/shard_map/pallas_call | solution.py:424
  119.5 5.2 %shard_map.109 = (bf16[512,512]{1,0:T(8,128)(2,1)S(1)}, bf16[512,512]{1,0:T(8,128)(2,1)S(1)}, bf16[1024,4096]{1,0:T(8,128)(2,1)S(1)}) custom-call(s32[32]{0:T(128)S(1)} %get-tuple-element.37.low_ref, s32[32]{0:T(128)S(1)} %get-tuple-element.38.high_ref, bf16[512,512]{1,0:T(8,128)(2,1)S(1)} %shard_map.103.refs_0_, ...), custom_call_target="tpu_custom_call" | custom-call | flops 536870912 | bytes 10000000 | tf_op jit(solution)/shard_map/pallas_call | solution.py:424
  133.5 4.0 %shard_map.111 = (bf16[128,1024]{1,0:T(8,128)(2,1)S(1)}, bf16[128,1024]{1,0:T(8,128)(2,1)S(1)}, bf16[128,1024]{1,0:T(8,128)(2,1)S(1)}, bf16[128,1024]{1,0:T(8,12...) custom-call(s32[1]{0:T(128)} %bitcast.core_ref, ...), custom_call_target="tpu_custom_call" | custom-call | flops 3221225472 | bytes 8388608 | tf_op jit(solution)/shard_map/pallas_call | solution.py:470
  138.8 5.5 %collective-permute-done.27 = bf16[128,1024]{1,0:T(8,128)(2,1)S(1)} collective-permute-done((bf16[128,1024]{1,0:T(8,128)(2,1)S(1)}, bf16[128,1024]{1,0:T(8,128)(2,1)S(1)}, u32[]{:S(2)}, u32[]{:S(2)}) %collective-permute-start.27) | collective-permute-done | bytes 262176 | tf_op jit(solution)/shard_map/ppermute | solution.py:63
  144.5 3.5 %collective-permute-start.31 = (bf16[128,1024]{1,0:T(8,128)(2,1)S(1)}, bf16[128,1024]{1,0:T(8,128)(2,1)S(1)}, u32[]{:S(2)}, u32[]{:S(2)}) collective-permute-start(bf16[128,1024]{1,0:T(8,128)(2,1)S(1)} %add_convert_fusion.3), channel_id=1, source_target_pairs={{0,3},{1,0},{2,1},{3,2},{4,7},{5,4},{6,5},{7,6},{8,11},{9,8},{10,9... | collective-permute-start | bytes 786440 | tf_op jit(solution)/shard_map/ppermute | solution.py:63
  150.4 5.1 %collective-permute-done.28 = bf16[128,1024]{1,0:T(8,128)(2,1)S(1)} collective-permute-done((bf16[128,1024]{1,0:T(8,128)(2,1)S(1)}, bf16[128,1024]{1,0:T(8,128)(2,1)S(1)}, u32[]{:S(2)}, u32[]{:S(2)}) %collective-permute-start.28) | collective-permute-done | bytes 262176 | tf_op jit(solution)/shard_map/ppermute | solution.py:63
  155.8 3.3 %collective-permute-start.32 = (bf16[128,1024]{1,0:T(8,128)(2,1)S(1)}, bf16[128,1024]{1,0:T(8,128)(2,1)S(1)}, u32[]{:S(2)}, u32[]{:S(2)}) collective-permute-start(bf16[128,1024]{1,0:T(8,128)(2,1)S(1)} %add_convert_fusion.2), channel_id=1, source_target_pairs={{0,3},{1,0},{2,1},{3,2},{4,7},{5,4},{6,5},{7,6},{8,11},{9,8},{10,9... | collective-permute-start | bytes 786440 | tf_op jit(solution)/shard_map/ppermute | solution.py:63
  161.8 4.2 %collective-permute-done.29 = bf16[128,1024]{1,0:T(8,128)(2,1)S(1)} collective-permute-done((bf16[128,1024]{1,0:T(8,128)(2,1)S(1)}, bf16[128,1024]{1,0:T(8,128)(2,1)S(1)}, u32[]{:S(2)}, u32[]{:S(2)}) %collective-permute-start.29) | collective-permute-done | bytes 262176 | tf_op jit(solution)/shard_map/ppermute | solution.py:63
  (159 shorter events, 59.4 us)
Async XLA Ops:
  3.9 42.9 %collective-permute-start.2 = (bf16[64,4096]{1,0:T(8,128)(2,1)S(1)}, bf16[64,4096]{1,0:T(8,128)(2,1)}, u32[]{:S(2)}, u32[]{:S(2)}) collective-permute-start(bf16[64,4096]{1,0:T(8,128)(2,1)S(1)} %get-tuple-element.39.refs_0_), channel_id=1, source_target_pairs={{0,3},{1,0},{2,1},{3,2},{4,7},{5,4},{6,5},{7,6},{8,11},{9,8},{10,9... | collective-permute-start | bytes 1572872 | tf_op jit(solution)/shard_map/ppermute | solution.py:63
  8.1 25.4 %collective-permute-start = (bf16[64,4096]{1,0:T(8,128)(2,1)S(1)}, bf16[64,4096]{1,0:T(8,128)(2,1)}, u32[]{:S(2)}, u32[]{:S(2)}) collective-permute-start(bf16[64,4096]{1,0:T(8,128)(2,1)S(1)} %get-tuple-element.39.refs_0_), channel_id=1, source_target_pairs={{0,1},{1,2},{2,3},{3,0},{4,5},{5,6},{6,7},{7,4},{8,9},{9,10},{10,1... | collective-permute-start | bytes 1572872 | tf_op jit(solution)/shard_map/ppermute | solution.py:63
  8.1 25.4 %collective-permute-start.3 = (bf16[64,4096]{1,0:T(8,128)(2,1)}, bf16[64,4096]{1,0:T(8,128)(2,1)}, u32[]{:S(2)}, u32[]{:S(2)}) collective-permute-start(bf16[64,4096]{1,0:T(8,128)(2,1)} %get-tuple-element.40.refs_1_), channel_id=1, source_target_pairs={{0,3},{1,0},{2,1},{3,2},{4,7},{5,4},{6,5},{7,6},{8,11},{9,8},{10,9... | collective-permute-start | bytes 1572872 | tf_op jit(solution)/shard_map/ppermute | solution.py:63
  11.3 35.5 %collective-permute-start.1 = (bf16[64,4096]{1,0:T(8,128)(2,1)}, bf16[64,4096]{1,0:T(8,128)(2,1)}, u32[]{:S(2)}, u32[]{:S(2)}) collective-permute-start(bf16[64,4096]{1,0:T(8,128)(2,1)} %get-tuple-element.40.refs_1_), channel_id=1, source_target_pairs={{0,1},{1,2},{2,3},{3,0},{4,5},{5,6},{6,7},{7,4},{8,9},{9,10},{10,1... | collective-permute-start | bytes 1572872 | tf_op jit(solution)/shard_map/ppermute | solution.py:63
  33.5 16.4 %collective-permute-start.4 = (bf16[64,4096]{1,0:T(8,128)(2,1)}, bf16[64,4096]{1,0:T(8,128)(2,1)}, u32[]{:S(2)}, u32[]{:S(2)}) collective-permute-start(bf16[64,4096]{1,0:T(8,128)(2,1)} %collective-permute-done.refs_2_.refs_0_), channel_id=1, source_target_pairs={{0,1},{1,2},{2,3},{3,0},{4,5},{5,6},{6,7},{7,4},{8,9},{9,10},{10,1... | collective-permute-start | bytes 1572872 | tf_op jit(solution)/shard_map/ppermute | solution.py:63
  33.5 16.4 %collective-permute-start.5 = (bf16[64,4096]{1,0:T(8,128)(2,1)}, bf16[64,4096]{1,0:T(8,128)(2,1)}, u32[]{:S(2)}, u32[]{:S(2)}) collective-permute-start(bf16[64,4096]{1,0:T(8,128)(2,1)} %collective-permute-done.3.refs_5_.refs_3_), channel_id=1, source_target_pairs={{0,3},{1,0},{2,1},{3,2},{4,7},{5,4},{6,5},{7,6},{8,11},{9,8},{10,9... | collective-permute-start | bytes 1572872 | tf_op jit(solution)/shard_map/ppermute | solution.py:63
  53.8 11.7 %collective-permute-start.13 = (bf16[2,512,256]{2,1,0:T(8,128)(2,1)S(1)}, bf16[2,512,256]{2,1,0:T(8,128)(2,1)S(1)}, u32[]{:S(2)}, u32[]{:S(2)}) collective-permute-start(bf16[2,512,256]{2,1,0:T(8,128)(2,1)S(1)} %pad_maximum_fusion.refs_4_), channel_id=1, source_target_pairs={{0,24},{1,25},{2,26},{3,27},{4,100},{5,101},{6,102},{7,103},{8,0},... | collective-permute-start | bytes 1572872 | tf_op jit(solution)/shard_map/ppermute | solution.py:63
  62.1 13.7 %collective-permute-start.21 = (bf16[2,512,256]{2,1,0:T(8,128)(2,1)S(1)}, bf16[2,512,256]{2,1,0:T(8,128)(2,1)S(1)}, u32[]{:S(2)}, u32[]{:S(2)}) collective-permute-start(bf16[2,512,256]{2,1,0:T(8,128)(2,1)S(1)} %pad_maximum_fusion.refs_4_), channel_id=1, source_target_pairs={{0,96},{1,97},{2,98},{3,99},{4,28},{5,29},{6,30},{7,31},{8,104},{9... | collective-permute-start | bytes 1572872 | tf_op jit(solution)/shard_map/ppermute | solution.py:63
  65.0 16.0 %collective-permute-start.10 = (bf16[2,512,256]{2,1,0:T(8,128)(2,1)S(1)}, bf16[2,512,256]{2,1,0:T(8,128)(2,1)S(1)}, u32[]{:S(2)}, u32[]{:S(2)}) collective-permute-start(bf16[2,512,256]{2,1,0:T(8,128)(2,1)S(1)} %pad_maximum_fusion.refs_4_), channel_id=1, source_target_pairs={{0,8},{1,9},{2,10},{3,11},{4,36},{5,37},{6,38},{7,39},{8,16},{9,17... | collective-permute-start | bytes 1572872 | tf_op jit(solution)/shard_map/ppermute | solution.py:63
  65.0 16.0 %collective-permute-start.8 = (bf16[2,512,256]{2,1,0:T(8,128)(2,1)S(1)}, bf16[2,512,256]{2,1,0:T(8,128)(2,1)}, u32[]{:S(2)}, u32[]{:S(2)}) collective-permute-start(bf16[2,512,256]{2,1,0:T(8,128)(2,1)S(1)} %pad_maximum_fusion.refs_4_), channel_id=1, source_target_pairs={{0,32},{1,33},{2,34},{3,35},{4,12},{5,13},{6,14},{7,15},{8,40},{9,... | collective-permute-start | bytes 1572872 | tf_op jit(solution)/shard_map/ppermute | solution.py:63
  65.6 18.3 %collective-permute-start.16 = (bf16[2,512,256]{2,1,0:T(8,128)(2,1)S(1)}, bf16[2,512,256]{2,1,0:T(8,128)(2,1)}, u32[]{:S(2)}, u32[]{:S(2)}) collective-permute-start(bf16[2,512,256]{2,1,0:T(8,128)(2,1)S(1)} %collective-permute-done.13.refs_6_), channel_id=1, source_target_pairs={{0,24},{1,25},{2,26},{3,27},{4,100},{5,101},{6,102},{7,103},{8,0},... | collective-permute-start | bytes 1572872 | tf_op jit(solution)/shard_map/ppermute | solution.py:63
  68.3 17.0 %collective-permute-start.19 = (bf16[2,512,256]{2,1,0:T(8,128)(2,1)S(1)}, bf16[2,512,256]{2,1,0:T(8,128)(2,1)S(1)}, u32[]{:S(2)}, u32[]{:S(2)}) collective-permute-start(bf16[2,512,256]{2,1,0:T(8,128)(2,1)S(1)} %collective-permute-done.13.refs_6_), channel_id=1, source_target_pairs={{0,32},{1,33},{2,34},{3,35},{4,12},{5,13},{6,14},{7,15},{8,40},{9,... | collective-permute-start | bytes 1572872 | tf_op jit(solution)/shard_map/ppermute | solution.py:63
  81.0 15.2 %collective-permute-start.11 = (bf16[2,512,256]{2,1,0:T(8,128)(2,1)S(1)}, bf16[2,512,256]{2,1,0:T(8,128)(2,1)}, u32[]{:S(2)}, u32[]{:S(2)}) collective-permute-start(bf16[2,512,256]{2,1,0:T(8,128)(2,1)S(1)} %collective-permute-done.10.refs_5_), channel_id=1, source_target_pairs={{0,32},{1,33},{2,34},{3,35},{4,12},{5,13},{6,14},{7,15},{8,40},{9,... | collective-permute-start | bytes 1572872 | tf_op jit(solution)/shard_map/ppermute | solution.py:63
  83.9 13.6 %collective-permute-start.17 = (bf16[2,512,256]{2,1,0:T(8,128)(2,1)}, bf16[2,512,256]{2,1,0:T(8,128)(2,1)}, u32[]{:S(2)}, u32[]{:S(2)}) collective-permute-start(bf16[2,512,256]{2,1,0:T(8,128)(2,1)} %collective-permute-done.16.refs_7_), channel_id=1, source_target_pairs={{0,96},{1,97},{2,98},{3,99},{4,28},{5,29},{6,30},{7,31},{8,104},{9... | collective-permute-start | bytes 1572872 | tf_op jit(solution)/shard_map/ppermute | solution.py:63
  86.1 23.8 %collective-permute-start.20 = (bf16[2,512,256]{2,1,0:T(8,128)(2,1)}, bf16[2,512,256]{2,1,0:T(8,128)(2,1)}, u32[]{:S(2)}, u32[]{:S(2)}) collective-permute-start(bf16[2,512,256]{2,1,0:T(8,128)(2,1)} %collective-permute-done.16.refs_7_), channel_id=1, source_target_pairs={{0,32},{1,33},{2,34},{3,35},{4,12},{5,13},{6,14},{7,15},{8,40},{9,... | collective-permute-start | bytes 1572872 | tf_op jit(solution)/shard_map/ppermute | solution.py:63
  86.7 32.8 %collective-permute-start.9 = (bf16[2,512,256]{2,1,0:T(8,128)(2,1)}, bf16[2,512,256]{2,1,0:T(8,128)(2,1)}, u32[]{:S(2)}, u32[]{:S(2)}) collective-permute-start(bf16[2,512,256]{2,1,0:T(8,128)(2,1)} %collective-permute-done.8.refs_8_), channel_id=1, source_target_pairs={{0,32},{1,33},{2,34},{3,35},{4,12},{5,13},{6,14},{7,15},{8,40},{9,... | collective-permute-start | bytes 1572872 | tf_op jit(solution)/shard_map/ppermute | solution.py:63
  92.5 26.9 %collective-permute-start.15 = (bf16[2,512,256]{2,1,0:T(8,128)(2,1)}, bf16[2,512,256]{2,1,0:T(8,128)(2,1)}, u32[]{:S(2)}, u32[]{:S(2)}) collective-permute-start(bf16[2,512,256]{2,1,0:T(8,128)(2,1)} %collective-permute-done.14.refs_14_), channel_id=1, source_target_pairs={{0,96},{1,97},{2,98},{3,99},{4,28},{5,29},{6,30},{7,31},{8,104},{9... | collective-permute-start | bytes 1572872 | tf_op jit(solution)/shard_map/ppermute | solution.py:63
  96.2 23.2 %collective-permute-start.12 = (bf16[2,512,256]{2,1,0:T(8,128)(2,1)}, bf16[2,512,256]{2,1,0:T(8,128)(2,1)}, u32[]{:S(2)}, u32[]{:S(2)}) collective-permute-start(bf16[2,512,256]{2,1,0:T(8,128)(2,1)} %collective-permute-done.11.refs_9_), channel_id=1, source_target_pairs={{0,32},{1,33},{2,34},{3,35},{4,12},{5,13},{6,14},{7,15},{8,40},{9,... | collective-permute-start | bytes 1572872 | tf_op jit(solution)/shard_map/ppermute | solution.py:63
  97.5 22.0 %collective-permute-start.18 = (bf16[2,512,256]{2,1,0:T(8,128)(2,1)}, bf16[2,512,256]{2,1,0:T(8,128)(2,1)}, u32[]{:S(2)}, u32[]{:S(2)}) collective-permute-start(bf16[2,512,256]{2,1,0:T(8,128)(2,1)} %collective-permute-done.17.refs_15_), channel_id=1, source_target_pairs={{0,96},{1,97},{2,98},{3,99},{4,28},{5,29},{6,30},{7,31},{8,104},{9... | collective-permute-start | bytes 1572872 | tf_op jit(solution)/shard_map/ppermute | solution.py:63
  128.3 16.0 %collective-permute-start.27 = (bf16[128,1024]{1,0:T(8,128)(2,1)S(1)}, bf16[128,1024]{1,0:T(8,128)(2,1)S(1)}, u32[]{:S(2)}, u32[]{:S(2)}) collective-permute-start(bf16[128,1024]{1,0:T(8,128)(2,1)S(1)} %get-tuple-element.57), channel_id=1, source_target_pairs={{0,1},{1,2},{2,3},{3,0},{4,5},{5,6},{6,7},{7,4},{8,9},{9,10},{10,1... | collective-permute-start | bytes 786440 | tf_op jit(solution)/shard_map/ppermute | solution.py:63
  129.6 14.8 %collective-permute-start.30 = (bf16[128,1024]{1,0:T(8,128)(2,1)S(1)}, bf16[128,1024]{1,0:T(8,128)(2,1)S(1)}, u32[]{:S(2)}, u32[]{:S(2)}) collective-permute-start(bf16[128,1024]{1,0:T(8,128)(2,1)S(1)} %get-tuple-element.61), channel_id=1, source_target_pairs={{0,3},{1,0},{2,1},{3,2},{4,7},{5,4},{6,5},{7,6},{8,11},{9,8},{10,9... | collective-permute-start | bytes 786440 | tf_op jit(solution)/shard_map/ppermute | solution.py:63
  131.6 16.5 %collective-permute-start.33 = (bf16[128,1024]{1,0:T(8,128)(2,1)S(1)}, bf16[128,1024]{1,0:T(8,128)(2,1)S(1)}, u32[]{:S(2)}, u32[]{:S(2)}) collective-permute-start(bf16[128,1024]{1,0:T(8,128)(2,1)S(1)} %get-tuple-element.65), channel_id=1, source_target_pairs={{0,3},{1,0},{2,1},{3,2},{4,7},{5,4},{6,5},{7,6},{8,11},{9,8},{10,9... | collective-permute-start | bytes 786440 | tf_op jit(solution)/shard_map/ppermute | solution.py:63
  144.4 11.2 %collective-permute-start.28 = (bf16[128,1024]{1,0:T(8,128)(2,1)S(1)}, bf16[128,1024]{1,0:T(8,128)(2,1)S(1)}, u32[]{:S(2)}, u32[]{:S(2)}) collective-permute-start(bf16[128,1024]{1,0:T(8,128)(2,1)S(1)} %add_convert_fusion.5), channel_id=1, source_target_pairs={{0,1},{1,2},{2,3},{3,0},{4,5},{5,6},{6,7},{7,4},{8,9},{9,10},{10,1... | collective-permute-start | bytes 786440 | tf_op jit(solution)/shard_map/ppermute | solution.py:63
  150.0 11.7 %collective-permute-start.26 = (bf16[128,1024]{1,0:T(8,128)(2,1)S(1)}, bf16[128,1024]{1,0:T(8,128)(2,1)S(1)}, u32[]{:S(2)}, u32[]{:S(2)}) collective-permute-start(bf16[128,1024]{1,0:T(8,128)(2,1)S(1)} %add_convert_fusion.6), channel_id=1, source_target_pairs={{0,1},{1,2},{2,3},{3,0},{4,5},{5,6},{6,7},{7,4},{8,9},{9,10},{10,1... | collective-permute-start | bytes 786440 | tf_op jit(solution)/shard_map/ppermute | solution.py:63
  (29 other events, 225.5 us)

commit v3 on v2

--- a/solution.py
+++ b/solution.py
@@ -265,9 +265,7 @@
                 [turn(both[:, :HEAD_DIM], cosine, sine), turn(both[:, HEAD_DIM:], cosine, sine)],
                 axis=1,
             )
-            turned_ref[at, first : first + 256] = (
-                turned * (HEAD_DIM ** (-0.5) * LOG2E)
-            ).astype(jnp.bfloat16)
+            turned_ref[at, first : first + 256] = turned.astype(jnp.bfloat16)
     out_ref[...] = jnp.dot(
         sorting(rank_ref[...]), turned_ref[...], preferred_element_type=jnp.float32
     ).astype(jnp.bfloat16)
@@ -298,6 +296,8 @@
         copy.start()
     else:
         (state_ref,) = refs
+
+    scale = HEAD_DIM ** (-0.5) * LOG2E
 
     def at(u, size):
         return pl.ds(pl.multiple_of(u * size, size), size)
@@ -341,7 +341,7 @@
             masked.append(jnp.where(allowed, score, score_floor))
         peaks = [spread(jnp.max(m, axis=1, keepdims=True)) for m in masked]
         peaks = [p if st is None else jnp.maximum(p, st[0]) for p, st in zip(peaks, states)]
-        weights = [jnp.exp2(m - spread(p, wide)) for m, p in zip(masked, peaks)]
+        weights = [jnp.exp2((m - spread(p, wide)) * scale) for m, p in zip(masked, peaks)]
         totals = [spread(jnp.sum(w, axis=1, keepdims=True)) for w in weights]
         mixes = [
             jnp.dot(w.astype(jnp.bfloat16), kv[:, HEAD_DIM:], preferred_element_type=jnp.float32)
@@ -350,7 +350,7 @@
         out = []
         for peak, total, mixed, st in zip(peaks, totals, mixes, states):
             if st is not None:
-                keep = jnp.exp2(st[0] - peak)
+                keep = jnp.exp2((st[0] - peak) * scale)
                 total = total + st[1] * keep
                 mixed = mixed + st[2] * keep
             out.append((peak, total, mixed))
@@ -454,6 +454,8 @@
             rows[block] = unsort(rank, block, (mine_ref, other_ref))
     for side in range(4):
         group = [(i, block) for i, (block, s) in enumerate(wanted) if s == side]
+        if not group:
+            continue
         mine = jnp.concatenate([rows[block][0] for _, block in group], axis=0)
         other = jnp.concatenate([rows[block][1] for _, block in group], axis=0)
         at = slice(side * part, (side + 1) * part)
@@ -604,29 +606,32 @@
     def plus(a, b):
         return a.astype(jnp.float32) + b.astype(jnp.float32)
 
-    ways = (along_z(1), along_z(1), along_z(-1), along_z(-1))
-    moving = products(
-        core_arg, rank_row, mine, other, w_near, ((1, 0), (1, 1), (2, 2), (2, 3))
-    )
-    moving = [send(a, way) for a, way in zip(moving, ways)]
+    ways = (along_z(1), along_z(-1)) * 2
+    first = products(core_arg, rank_row, mine, other, w_near, ((1, 0), (2, 2)))
+    early = [send(a, way) for a, way in zip(first, ways)]
+    sides = (0, 2, 1, 3)
     terms = products(
         core_arg,
         rank_row,
         mine,
         other,
         w_near,
-        tuple(
+        ((1, 1), (2, 3))
+        + tuple(
             (block, side)
-            for blocks in ((3, 3, 3, 3), (2, 2, 1, 1), (0, 0, 0, 0))
-            for side, block in enumerate(blocks)
+            for blocks in ((3, 3, 3, 3), (2, 1, 2, 1), (0, 0, 0, 0))
+            for side, block in zip(sides, blocks)
         ),
     )
-    for first in (0, 4):
+    late = [send(a, way) for a, way in zip(terms[:2], ways)]
+    moving = early + late
+    for first in (2, 6):
         moving = [
             send(plus(a, b).astype(jnp.bfloat16), way)
             for a, b, way in zip(moving, terms[first : first + 4], ways)
         ]
-    attended = jnp.concatenate([plus(a, b) for a, b in zip(moving, terms[8:])], axis=1)
+    attended = [plus(a, b) for a, b in zip(moving, terms[10:])]
+    attended = jnp.concatenate([attended[n] for n in (0, 2, 1, 3)], axis=1)
     return (tokens.astype(jnp.float32) + attended).astype(jnp.bfloat16)
 
 

time: 171 us -> 169 us (0.988)
  waiting for transfers between devices: 38.6 us -> 32 us
  starting transfers between devices: 51.4 us -> 56.2 us
    ppermute x36, waiting for transfers between devices: 38.6 us -> 32 us  [send(): return lax.ppermute(array, AXES, moves)]
    ppermute x36, starting transfers between devices: 51.4 us -> 56.2 us  [send(): return lax.ppermute(array, AXES, moves)]
  transfers between devices with their start and end apart: 36 -> 36, of which waited for: 13 -> 12; matrix products, arithmetic and copies ran while one was open for 9% -> 9% of each run, Pallas kernels for 25% -> 26%
where the time goes in v3:
time: 169 us
  starting transfers between devices  56.2 us (33%)
  Pallas kernels  53.9 us (32%)
  waiting for transfers between devices  32 us (19%)
  local copies, waits for them, and re-layouts  13.5 us (8%)
  other arithmetic  12.6 us (7%)
    ppermute x36, starting transfers between devices, send(): return lax.ppermute(array, AXES, moves)  56.2 us
    ppermute x36, waiting for transfers between devices, send(): return lax.ppermute(array, AXES, moves)  32 us
    pallas_call x2, Pallas kernels, attend(): pl.pallas_call(functools.partial(attend_kernel, opening, closing, batch,...  15.2 us
    pallas_call x1, Pallas kernels, order_groups(): pl.pallas_call(order_kernel, out_shape=jax.ShapeDtypeStruct((GROUPS, ROWS...  10.6 us
    pallas_call x2, Pallas kernels, project_q(): pl.pallas_call(functools.partial(q_kernel, len(pieces), mine), out_shape=...  10 us
    unnamed x34, local copies, waits for them, and re-layouts  9.09 us
    pallas_call x2, Pallas kernels, products(): pl.pallas_call(functools.partial(product_kernel, wanted), out_shape=[shap...  5.61 us
    pallas_call x2, Pallas kernels, project_kv(): pl.pallas_call(functools.partial(kv_kernel, len(pieces), first), out_shap...  5.03 us
  transfers between devices with their start and end apart: 36, of which 12 were waited for; matrix products, arithmetic and copies ran while one was open for 9% of the time, Pallas kernels for 26%

profile of v3, /device:TPU:0, one launch (start us, length us, event | category | flops | bytes accessed | tf_op | source)
XLA Modules:
  0.0 168.8 jit_solution(8065585783693105842)
XLA Ops:
  3.9 4.1 %collective-permute-start.2 = (bf16[64,4096]{1,0:T(8,128)(2,1)S(1)}, bf16[64,4096]{1,0:T(8,128)(2,1)}, u32[]{:S(2)}, u32[]{:S(2)}) collective-permute-start(bf16[64,4096]{1,0:T(8,128)(2,1)S(1)} %get-tuple-element.39.refs_0_), channel_id=1, source_target_pairs={{0,3},{1,0},{2,1},{3,2},{4,7},{5,4},{6,5},{7,6},{8,11},{9,8},{10,9... | collective-permute-start | bytes 1572872 | tf_op jit(solution)/shard_map/ppermute | solution.py:63
  8.1 3.2 %collective-permute-start.3 = (bf16[64,4096]{1,0:T(8,128)(2,1)}, bf16[64,4096]{1,0:T(8,128)(2,1)}, u32[]{:S(2)}, u32[]{:S(2)}) collective-permute-start(bf16[64,4096]{1,0:T(8,128)(2,1)} %get-tuple-element.40.refs_1_), channel_id=1, source_target_pairs={{0,3},{1,0},{2,1},{3,2},{4,7},{5,4},{6,5},{7,6},{8,11},{9,8},{10,9... | collective-permute-start | bytes 1572872 | tf_op jit(solution)/shard_map/ppermute | solution.py:63
  16.4 10.6 %shard_map.100 = f32[32,512]{1,0:T(8,128)S(1)} custom-call(f32[32,512]{1,0:T(8,128)S(1)} %convert_element_type.136.packed_ref), custom_call_target="tpu_custom_call" | custom-call | flops 50331648 | bytes 131072 | tf_op jit(solution)/shard_map/pallas_call | solution.py:143
  33.5 3.3 %collective-permute-start.5 = (bf16[64,4096]{1,0:T(8,128)(2,1)}, bf16[64,4096]{1,0:T(8,128)(2,1)}, u32[]{:S(2)}, u32[]{:S(2)}) collective-permute-start(bf16[64,4096]{1,0:T(8,128)(2,1)} %collective-permute-done.3.refs_5_.refs_3_), channel_id=1, source_target_pairs={{0,3},{1,0},{2,1},{3,2},{4,7},{5,4},{6,5},{7,6},{8,11},{9,8},{10,9... | collective-permute-start | bytes 1572872 | tf_op jit(solution)/shard_map/ppermute | solution.py:63
  38.5 3.2 %shard_map.101.refs_3_ = s32[4096,128]{1,0:T(8,128)S(1)} custom-call(s32[32,128]{1,0:T(8,128)S(1)} %copy.21.packed_ref), custom_call_target="tpu_custom_call" | custom-call | flops 16777216 | bytes 2097152 | tf_op jit(solution)/shard_map/pallas_call | solution.py:163
  56.9 4.9 %shard_map.104 = bf16[512,512]{1,0:T(8,128)(2,1)S(1)} custom-call(s32[1]{0:T(128)} %bitcast.core_ref, bf16[64,4096]{1,0:T(8,128)(2,1)S(1)} %get-tuple-element.39.refs_0_, bf16[64,4096]{1,0:T(8,128)(2,1)} %get-tuple-element.40.refs_1_, bf16[64,4096]{1,0:T(8,128)(2,1)} %collective-permute-done.refs_2_.refs_0_, ...), custom_call_target="tpu_custom_call" | custom-call | flops 2147483648 | bytes 8388608 | tf_op jit(solution)/shard_map/pallas_call | solution.py:276
  69.0 6.6 %collective-permute-done.21.refs_12_ = bf16[2,512,256]{2,1,0:T(8,128)(2,1)S(1)} collective-permute-done((bf16[2,512,256]{2,1,0:T(8,128)(2,1)S(1)}, bf16[2,512,256]{2,1,0:T(8,128)(2,1)S(1)}, u32[]{:S(2)}, u32[]{:S(2)}) %collective-permute-start.21) | collective-permute-done | bytes 524320 | tf_op jit(solution)/shard_map/ppermute | solution.py:63
  75.7 3.7 %collective-permute-start.14 = (bf16[2,512,256]{2,1,0:T(8,128)(2,1)S(1)}, bf16[2,512,256]{2,1,0:T(8,128)(2,1)}, u32[]{:S(2)}, u32[]{:S(2)}) collective-permute-start(bf16[2,512,256]{2,1,0:T(8,128)(2,1)S(1)} %collective-permute-done.13.refs_6_), channel_id=1, source_target_pairs={{0,96},{1,97},{2,98},{3,99},{4,28},{5,29},{6,30},{7,31},{8,104},{9... | collective-permute-start | bytes 1572872 | tf_op jit(solution)/shard_map/ppermute | solution.py:63
  86.7 5.0 %collective-permute-done.22.refs_13_ = bf16[2,512,256]{2,1,0:T(8,128)(2,1)S(1)} collective-permute-done((bf16[2,512,256]{2,1,0:T(8,128)(2,1)S(1)}, bf16[2,512,256]{2,1,0:T(8,128)(2,1)S(1)}, u32[]{:S(2)}, u32[]{:S(2)}) %collective-permute-start.22) | collective-permute-done | bytes 524320 | tf_op jit(solution)/shard_map/ppermute | solution.py:63
  92.5 3.7 %collective-permute-start.15 = (bf16[2,512,256]{2,1,0:T(8,128)(2,1)}, bf16[2,512,256]{2,1,0:T(8,128)(2,1)}, u32[]{:S(2)}, u32[]{:S(2)}) collective-permute-start(bf16[2,512,256]{2,1,0:T(8,128)(2,1)} %collective-permute-done.14.refs_14_), channel_id=1, source_target_pairs={{0,96},{1,97},{2,98},{3,99},{4,28},{5,29},{6,30},{7,31},{8,104},{9... | collective-permute-start | bytes 1572872 | tf_op jit(solution)/shard_map/ppermute | solution.py:63
  97.4 3.7 %collective-permute-start.18 = (bf16[2,512,256]{2,1,0:T(8,128)(2,1)}, bf16[2,512,256]{2,1,0:T(8,128)(2,1)}, u32[]{:S(2)}, u32[]{:S(2)}) collective-permute-start(bf16[2,512,256]{2,1,0:T(8,128)(2,1)} %collective-permute-done.17.refs_15_), channel_id=1, source_target_pairs={{0,96},{1,97},{2,98},{3,99},{4,28},{5,29},{6,30},{7,31},{8,104},{9... | collective-permute-start | bytes 1572872 | tf_op jit(solution)/shard_map/ppermute | solution.py:63
  101.3 3.4 %copy-done = bf16[4096,1024]{1,0:T(8,128)(2,1)S(1)} copy-done((bf16[4096,1024]{1,0:T(8,128)(2,1)S(1)}, bf16[4096,1024]{1,0:T(8,128)(2,1)}, u32[]{:S(2)}) %copy-start) | copy-done | bytes 8388632
  104.7 5.1 %shard_map.103.refs_0_ = bf16[512,512]{1,0:T(8,128)(2,1)S(1)} custom-call(s32[1]{0:T(128)} %bitcast.core_ref, bf16[64,4096]{1,0:T(8,128)(2,1)S(1)} %get-tuple-element.39.refs_0_, bf16[64,4096]{1,0:T(8,128)(2,1)} %get-tuple-element.40.refs_1_, bf16[64,4096]{1,0:T(8,128)(2,1)} %collective-permute-done.refs_2_.refs_0_, ...), custom_call_target="tpu_custom_call" | custom-call | flops 2147483648 | bytes 8388608 | tf_op jit(solution)/shard_map/pallas_call | solution.py:276
  109.8 9.9 %shard_map.108.refs_8_ = f32[4096,384]{1,0:T(8,128)S(1)} custom-call(s32[32]{0:T(128)S(1)} %get-tuple-element.47.low_ref, s32[32]{0:T(128)S(1)} %get-tuple-element.48.high_ref, bf16[512,512]{1,0:T(8,128)(2,1)S(1)} %shard_map.103.refs_0_, bf16[512,512]{1,0:T(8,128)(2,1)S(1)} %collective-permute-done.6.refs_1_, s32[32,384]{1,0:T(8,128)S(1)} %copy.25.refs_2_, ...), custom_call_target="tpu_custom_call" | custom-call | flops 1610612736 | bytes 10000000 | tf_op jit(solution)/shard_map/pallas_call | solution.py:424
  119.8 5.3 %shard_map.109 = (bf16[512,512]{1,0:T(8,128)(2,1)S(1)}, bf16[512,512]{1,0:T(8,128)(2,1)S(1)}, bf16[1024,4096]{1,0:T(8,128)(2,1)S(1)}) custom-call(s32[32]{0:T(128)S(1)} %get-tuple-element.37.low_ref, s32[32]{0:T(128)S(1)} %get-tuple-element.38.high_ref, bf16[512,512]{1,0:T(8,128)(2,1)S(1)} %shard_map.103.refs_0_, ...), custom_call_target="tpu_custom_call" | custom-call | flops 536870912 | bytes 10000000 | tf_op jit(solution)/shard_map/pallas_call | solution.py:424
  128.2 3.2 %collective-permute-start.30 = (bf16[128,1024]{1,0:T(8,128)(2,1)S(1)}, bf16[128,1024]{1,0:T(8,128)(2,1)S(1)}, u32[]{:S(2)}, u32[]{:S(2)}) collective-permute-start(bf16[128,1024]{1,0:T(8,128)(2,1)S(1)} %get-tuple-element.61), channel_id=1, source_target_pairs={{0,3},{1,0},{2,1},{3,2},{4,7},{5,4},{6,5},{7,6},{8,11},{9,8},{10,9... | collective-permute-start | bytes 786440 | tf_op jit(solution)/shard_map/ppermute | solution.py:63
  131.4 4.6 %shard_map.111 = (bf16[128,1024]{1,0:T(8,128)(2,1)S(1)}, bf16[128,1024]{1,0:T(8,128)(2,1)S(1)}, bf16[128,1024]{1,0:T(8,128)(2,1)S(1)}, bf16[128,1024]{1,0:T(8,12...) custom-call(s32[1]{0:T(128)} %bitcast.core_ref, ...), custom_call_target="tpu_custom_call" | custom-call | flops 3758096384 | bytes 8388608 | tf_op jit(solution)/shard_map/pallas_call | solution.py:472
  136.1 3.2 %collective-permute-start.33 = (bf16[128,1024]{1,0:T(8,128)(2,1)S(1)}, bf16[128,1024]{1,0:T(8,128)(2,1)S(1)}, u32[]{:S(2)}, u32[]{:S(2)}) collective-permute-start(bf16[128,1024]{1,0:T(8,128)(2,1)S(1)} %get-tuple-element.65), channel_id=1, source_target_pairs={{0,3},{1,0},{2,1},{3,2},{4,7},{5,4},{6,5},{7,6},{8,11},{9,8},{10,9... | collective-permute-start | bytes 786440 | tf_op jit(solution)/shard_map/ppermute | solution.py:63
  139.5 3.3 %collective-permute-start.31 = (bf16[128,1024]{1,0:T(8,128)(2,1)S(1)}, bf16[128,1024]{1,0:T(8,128)(2,1)S(1)}, u32[]{:S(2)}, u32[]{:S(2)}) collective-permute-start(bf16[128,1024]{1,0:T(8,128)(2,1)S(1)} %add_convert_fusion.3), channel_id=1, source_target_pairs={{0,3},{1,0},{2,1},{3,2},{4,7},{5,4},{6,5},{7,6},{8,11},{9,8},{10,9... | collective-permute-start | bytes 786440 | tf_op jit(solution)/shard_map/ppermute | solution.py:63
  142.8 3.6 %collective-permute-done.27 = bf16[128,1024]{1,0:T(8,128)(2,1)S(1)} collective-permute-done((bf16[128,1024]{1,0:T(8,128)(2,1)S(1)}, bf16[128,1024]{1,0:T(8,128)(2,1)S(1)}, u32[]{:S(2)}, u32[]{:S(2)}) %collective-permute-start.27) | collective-permute-done | bytes 262176 | tf_op jit(solution)/shard_map/ppermute | solution.py:63
  146.9 3.3 %collective-permute-start.34 = (bf16[128,1024]{1,0:T(8,128)(2,1)S(1)}, bf16[128,1024]{1,0:T(8,128)(2,1)S(1)}, u32[]{:S(2)}, u32[]{:S(2)}) collective-permute-start(bf16[128,1024]{1,0:T(8,128)(2,1)S(1)} %add_convert_fusion.1), channel_id=1, source_target_pairs={{0,3},{1,0},{2,1},{3,2},{4,7},{5,4},{6,5},{7,6},{8,11},{9,8},{10,9... | collective-permute-start | bytes 786440 | tf_op jit(solution)/shard_map/ppermute | solution.py:63
  152.3 3.3 %collective-permute-start.32 = (bf16[128,1024]{1,0:T(8,128)(2,1)S(1)}, bf16[128,1024]{1,0:T(8,128)(2,1)S(1)}, u32[]{:S(2)}, u32[]{:S(2)}) collective-permute-start(bf16[128,1024]{1,0:T(8,128)(2,1)S(1)} %add_convert_fusion.2), channel_id=1, source_target_pairs={{0,3},{1,0},{2,1},{3,2},{4,7},{5,4},{6,5},{7,6},{8,11},{9,8},{10,9... | collective-permute-start | bytes 786440 | tf_op jit(solution)/shard_map/ppermute | solution.py:63
  157.9 3.3 %collective-permute-start.35 = (bf16[128,1024]{1,0:T(8,128)(2,1)S(1)}, bf16[128,1024]{1,0:T(8,128)(2,1)S(1)}, u32[]{:S(2)}, u32[]{:S(2)}) collective-permute-start(bf16[128,1024]{1,0:T(8,128)(2,1)S(1)} %add_convert_fusion), channel_id=1, source_target_pairs={{0,3},{1,0},{2,1},{3,2},{4,7},{5,4},{6,5},{7,6},{8,11},{9,8},{10,9... | collective-permute-start | bytes 786440 | tf_op jit(solution)/shard_map/ppermute | solution.py:63
  163.4 4.1 %collective-permute-done.29 = bf16[128,1024]{1,0:T(8,128)(2,1)S(1)} collective-permute-done((bf16[128,1024]{1,0:T(8,128)(2,1)S(1)}, bf16[128,1024]{1,0:T(8,128)(2,1)S(1)}, u32[]{:S(2)}, u32[]{:S(2)}) %collective-permute-start.29) | collective-permute-done | bytes 262176 | tf_op jit(solution)/shard_map/ppermute | solution.py:63
  (159 shorter events, 60.6 us)
Async XLA Ops:
  3.9 42.9 %collective-permute-start.2 = (bf16[64,4096]{1,0:T(8,128)(2,1)S(1)}, bf16[64,4096]{1,0:T(8,128)(2,1)}, u32[]{:S(2)}, u32[]{:S(2)}) collective-permute-start(bf16[64,4096]{1,0:T(8,128)(2,1)S(1)} %get-tuple-element.39.refs_0_), channel_id=1, source_target_pairs={{0,3},{1,0},{2,1},{3,2},{4,7},{5,4},{6,5},{7,6},{8,11},{9,8},{10,9... | collective-permute-start | bytes 1572872 | tf_op jit(solution)/shard_map/ppermute | solution.py:63
  8.1 25.4 %collective-permute-start = (bf16[64,4096]{1,0:T(8,128)(2,1)S(1)}, bf16[64,4096]{1,0:T(8,128)(2,1)}, u32[]{:S(2)}, u32[]{:S(2)}) collective-permute-start(bf16[64,4096]{1,0:T(8,128)(2,1)S(1)} %get-tuple-element.39.refs_0_), channel_id=1, source_target_pairs={{0,1},{1,2},{2,3},{3,0},{4,5},{5,6},{6,7},{7,4},{8,9},{9,10},{10,1... | collective-permute-start | bytes 1572872 | tf_op jit(solution)/shard_map/ppermute | solution.py:63
  8.1 25.4 %collective-permute-start.3 = (bf16[64,4096]{1,0:T(8,128)(2,1)}, bf16[64,4096]{1,0:T(8,128)(2,1)}, u32[]{:S(2)}, u32[]{:S(2)}) collective-permute-start(bf16[64,4096]{1,0:T(8,128)(2,1)} %get-tuple-element.40.refs_1_), channel_id=1, source_target_pairs={{0,3},{1,0},{2,1},{3,2},{4,7},{5,4},{6,5},{7,6},{8,11},{9,8},{10,9... | collective-permute-start | bytes 1572872 | tf_op jit(solution)/shard_map/ppermute | solution.py:63
  11.3 35.5 %collective-permute-start.1 = (bf16[64,4096]{1,0:T(8,128)(2,1)}, bf16[64,4096]{1,0:T(8,128)(2,1)}, u32[]{:S(2)}, u32[]{:S(2)}) collective-permute-start(bf16[64,4096]{1,0:T(8,128)(2,1)} %get-tuple-element.40.refs_1_), channel_id=1, source_target_pairs={{0,1},{1,2},{2,3},{3,0},{4,5},{5,6},{6,7},{7,4},{8,9},{9,10},{10,1... | collective-permute-start | bytes 1572872 | tf_op jit(solution)/shard_map/ppermute | solution.py:63
  33.5 16.4 %collective-permute-start.4 = (bf16[64,4096]{1,0:T(8,128)(2,1)}, bf16[64,4096]{1,0:T(8,128)(2,1)}, u32[]{:S(2)}, u32[]{:S(2)}) collective-permute-start(bf16[64,4096]{1,0:T(8,128)(2,1)} %collective-permute-done.refs_2_.refs_0_), channel_id=1, source_target_pairs={{0,1},{1,2},{2,3},{3,0},{4,5},{5,6},{6,7},{7,4},{8,9},{9,10},{10,1... | collective-permute-start | bytes 1572872 | tf_op jit(solution)/shard_map/ppermute | solution.py:63
  33.5 16.4 %collective-permute-start.5 = (bf16[64,4096]{1,0:T(8,128)(2,1)}, bf16[64,4096]{1,0:T(8,128)(2,1)}, u32[]{:S(2)}, u32[]{:S(2)}) collective-permute-start(bf16[64,4096]{1,0:T(8,128)(2,1)} %collective-permute-done.3.refs_5_.refs_3_), channel_id=1, source_target_pairs={{0,3},{1,0},{2,1},{3,2},{4,7},{5,4},{6,5},{7,6},{8,11},{9,8},{10,9... | collective-permute-start | bytes 1572872 | tf_op jit(solution)/shard_map/ppermute | solution.py:63
  53.8 11.8 %collective-permute-start.13 = (bf16[2,512,256]{2,1,0:T(8,128)(2,1)S(1)}, bf16[2,512,256]{2,1,0:T(8,128)(2,1)S(1)}, u32[]{:S(2)}, u32[]{:S(2)}) collective-permute-start(bf16[2,512,256]{2,1,0:T(8,128)(2,1)S(1)} %pad_maximum_fusion.refs_4_), channel_id=1, source_target_pairs={{0,24},{1,25},{2,26},{3,27},{4,100},{5,101},{6,102},{7,103},{8,0},... | collective-permute-start | bytes 1572872 | tf_op jit(solution)/shard_map/ppermute | solution.py:63
  62.1 13.6 %collective-permute-start.21 = (bf16[2,512,256]{2,1,0:T(8,128)(2,1)S(1)}, bf16[2,512,256]{2,1,0:T(8,128)(2,1)S(1)}, u32[]{:S(2)}, u32[]{:S(2)}) collective-permute-start(bf16[2,512,256]{2,1,0:T(8,128)(2,1)S(1)} %pad_maximum_fusion.refs_4_), channel_id=1, source_target_pairs={{0,96},{1,97},{2,98},{3,99},{4,28},{5,29},{6,30},{7,31},{8,104},{9... | collective-permute-start | bytes 1572872 | tf_op jit(solution)/shard_map/ppermute | solution.py:63
  65.0 16.0 %collective-permute-start.10 = (bf16[2,512,256]{2,1,0:T(8,128)(2,1)S(1)}, bf16[2,512,256]{2,1,0:T(8,128)(2,1)S(1)}, u32[]{:S(2)}, u32[]{:S(2)}) collective-permute-start(bf16[2,512,256]{2,1,0:T(8,128)(2,1)S(1)} %pad_maximum_fusion.refs_4_), channel_id=1, source_target_pairs={{0,8},{1,9},{2,10},{3,11},{4,36},{5,37},{6,38},{7,39},{8,16},{9,17... | collective-permute-start | bytes 1572872 | tf_op jit(solution)/shard_map/ppermute | solution.py:63
  65.0 16.0 %collective-permute-start.8 = (bf16[2,512,256]{2,1,0:T(8,128)(2,1)S(1)}, bf16[2,512,256]{2,1,0:T(8,128)(2,1)}, u32[]{:S(2)}, u32[]{:S(2)}) collective-permute-start(bf16[2,512,256]{2,1,0:T(8,128)(2,1)S(1)} %pad_maximum_fusion.refs_4_), channel_id=1, source_target_pairs={{0,32},{1,33},{2,34},{3,35},{4,12},{5,13},{6,14},{7,15},{8,40},{9,... | collective-permute-start | bytes 1572872 | tf_op jit(solution)/shard_map/ppermute | solution.py:63
  65.6 18.2 %collective-permute-start.16 = (bf16[2,512,256]{2,1,0:T(8,128)(2,1)S(1)}, bf16[2,512,256]{2,1,0:T(8,128)(2,1)}, u32[]{:S(2)}, u32[]{:S(2)}) collective-permute-start(bf16[2,512,256]{2,1,0:T(8,128)(2,1)S(1)} %collective-permute-done.13.refs_6_), channel_id=1, source_target_pairs={{0,24},{1,25},{2,26},{3,27},{4,100},{5,101},{6,102},{7,103},{8,0},... | collective-permute-start | bytes 1572872 | tf_op jit(solution)/shard_map/ppermute | solution.py:63
  68.2 17.1 %collective-permute-start.19 = (bf16[2,512,256]{2,1,0:T(8,128)(2,1)S(1)}, bf16[2,512,256]{2,1,0:T(8,128)(2,1)S(1)}, u32[]{:S(2)}, u32[]{:S(2)}) collective-permute-start(bf16[2,512,256]{2,1,0:T(8,128)(2,1)S(1)} %collective-permute-done.13.refs_6_), channel_id=1, source_target_pairs={{0,32},{1,33},{2,34},{3,35},{4,12},{5,13},{6,14},{7,15},{8,40},{9,... | collective-permute-start | bytes 1572872 | tf_op jit(solution)/shard_map/ppermute | solution.py:63
  81.0 15.2 %collective-permute-start.11 = (bf16[2,512,256]{2,1,0:T(8,128)(2,1)S(1)}, bf16[2,512,256]{2,1,0:T(8,128)(2,1)}, u32[]{:S(2)}, u32[]{:S(2)}) collective-permute-start(bf16[2,512,256]{2,1,0:T(8,128)(2,1)S(1)} %collective-permute-done.10.refs_5_), channel_id=1, source_target_pairs={{0,32},{1,33},{2,34},{3,35},{4,12},{5,13},{6,14},{7,15},{8,40},{9,... | collective-permute-start | bytes 1572872 | tf_op jit(solution)/shard_map/ppermute | solution.py:63
  83.8 13.6 %collective-permute-start.17 = (bf16[2,512,256]{2,1,0:T(8,128)(2,1)}, bf16[2,512,256]{2,1,0:T(8,128)(2,1)}, u32[]{:S(2)}, u32[]{:S(2)}) collective-permute-start(bf16[2,512,256]{2,1,0:T(8,128)(2,1)} %collective-permute-done.16.refs_7_), channel_id=1, source_target_pairs={{0,96},{1,97},{2,98},{3,99},{4,28},{5,29},{6,30},{7,31},{8,104},{9... | collective-permute-start | bytes 1572872 | tf_op jit(solution)/shard_map/ppermute | solution.py:63
  86.1 23.7 %collective-permute-start.20 = (bf16[2,512,256]{2,1,0:T(8,128)(2,1)}, bf16[2,512,256]{2,1,0:T(8,128)(2,1)}, u32[]{:S(2)}, u32[]{:S(2)}) collective-permute-start(bf16[2,512,256]{2,1,0:T(8,128)(2,1)} %collective-permute-done.16.refs_7_), channel_id=1, source_target_pairs={{0,32},{1,33},{2,34},{3,35},{4,12},{5,13},{6,14},{7,15},{8,40},{9,... | collective-permute-start | bytes 1572872 | tf_op jit(solution)/shard_map/ppermute | solution.py:63
  86.6 33.1 %collective-permute-start.9 = (bf16[2,512,256]{2,1,0:T(8,128)(2,1)}, bf16[2,512,256]{2,1,0:T(8,128)(2,1)}, u32[]{:S(2)}, u32[]{:S(2)}) collective-permute-start(bf16[2,512,256]{2,1,0:T(8,128)(2,1)} %collective-permute-done.8.refs_8_), channel_id=1, source_target_pairs={{0,32},{1,33},{2,34},{3,35},{4,12},{5,13},{6,14},{7,15},{8,40},{9,... | collective-permute-start | bytes 1572872 | tf_op jit(solution)/shard_map/ppermute | solution.py:63
  92.5 27.2 %collective-permute-start.15 = (bf16[2,512,256]{2,1,0:T(8,128)(2,1)}, bf16[2,512,256]{2,1,0:T(8,128)(2,1)}, u32[]{:S(2)}, u32[]{:S(2)}) collective-permute-start(bf16[2,512,256]{2,1,0:T(8,128)(2,1)} %collective-permute-done.14.refs_14_), channel_id=1, source_target_pairs={{0,96},{1,97},{2,98},{3,99},{4,28},{5,29},{6,30},{7,31},{8,104},{9... | collective-permute-start | bytes 1572872 | tf_op jit(solution)/shard_map/ppermute | solution.py:63
  96.2 23.6 %collective-permute-start.12 = (bf16[2,512,256]{2,1,0:T(8,128)(2,1)}, bf16[2,512,256]{2,1,0:T(8,128)(2,1)}, u32[]{:S(2)}, u32[]{:S(2)}) collective-permute-start(bf16[2,512,256]{2,1,0:T(8,128)(2,1)} %collective-permute-done.11.refs_9_), channel_id=1, source_target_pairs={{0,32},{1,33},{2,34},{3,35},{4,12},{5,13},{6,14},{7,15},{8,40},{9,... | collective-permute-start | bytes 1572872 | tf_op jit(solution)/shard_map/ppermute | solution.py:63
  97.4 22.3 %collective-permute-start.18 = (bf16[2,512,256]{2,1,0:T(8,128)(2,1)}, bf16[2,512,256]{2,1,0:T(8,128)(2,1)}, u32[]{:S(2)}, u32[]{:S(2)}) collective-permute-start(bf16[2,512,256]{2,1,0:T(8,128)(2,1)} %collective-permute-done.17.refs_15_), channel_id=1, source_target_pairs={{0,96},{1,97},{2,98},{3,99},{4,28},{5,29},{6,30},{7,31},{8,104},{9... | collective-permute-start | bytes 1572872 | tf_op jit(solution)/shard_map/ppermute | solution.py:63
  128.1 11.2 %collective-permute-start.24 = (bf16[128,1024]{1,0:T(8,128)(2,1)S(1)}, bf16[128,1024]{1,0:T(8,128)(2,1)S(1)}, u32[]{:S(2)}, u32[]{:S(2)}) collective-permute-start(bf16[128,1024]{1,0:T(8,128)(2,1)S(1)} %get-tuple-element.53), channel_id=1, source_target_pairs={{0,1},{1,2},{2,3},{3,0},{4,5},{5,6},{6,7},{7,4},{8,9},{9,10},{10,1... | collective-permute-start | bytes 786440 | tf_op jit(solution)/shard_map/ppermute | solution.py:63
  128.2 11.3 %collective-permute-start.30 = (bf16[128,1024]{1,0:T(8,128)(2,1)S(1)}, bf16[128,1024]{1,0:T(8,128)(2,1)S(1)}, u32[]{:S(2)}, u32[]{:S(2)}) collective-permute-start(bf16[128,1024]{1,0:T(8,128)(2,1)S(1)} %get-tuple-element.61), channel_id=1, source_target_pairs={{0,3},{1,0},{2,1},{3,2},{4,7},{5,4},{6,5},{7,6},{8,11},{9,8},{10,9... | collective-permute-start | bytes 786440 | tf_op jit(solution)/shard_map/ppermute | solution.py:63
  139.4 12.7 %collective-permute-start.25 = (bf16[128,1024]{1,0:T(8,128)(2,1)S(1)}, bf16[128,1024]{1,0:T(8,128)(2,1)S(1)}, u32[]{:S(2)}, u32[]{:S(2)}) collective-permute-start(bf16[128,1024]{1,0:T(8,128)(2,1)S(1)} %add_convert_fusion.7), channel_id=1, source_target_pairs={{0,1},{1,2},{2,3},{3,0},{4,5},{5,6},{6,7},{7,4},{8,9},{9,10},{10,1... | collective-permute-start | bytes 786440 | tf_op jit(solution)/shard_map/ppermute | solution.py:63
  139.5 12.7 %collective-permute-start.31 = (bf16[128,1024]{1,0:T(8,128)(2,1)S(1)}, bf16[128,1024]{1,0:T(8,128)(2,1)S(1)}, u32[]{:S(2)}, u32[]{:S(2)}) collective-permute-start(bf16[128,1024]{1,0:T(8,128)(2,1)S(1)} %add_convert_fusion.3), channel_id=1, source_target_pairs={{0,3},{1,0},{2,1},{3,2},{4,7},{5,4},{6,5},{7,6},{8,11},{9,8},{10,9... | collective-permute-start | bytes 786440 | tf_op jit(solution)/shard_map/ppermute | solution.py:63
  146.5 11.2 %collective-permute-start.28 = (bf16[128,1024]{1,0:T(8,128)(2,1)S(1)}, bf16[128,1024]{1,0:T(8,128)(2,1)S(1)}, u32[]{:S(2)}, u32[]{:S(2)}) collective-permute-start(bf16[128,1024]{1,0:T(8,128)(2,1)S(1)} %add_convert_fusion.5), channel_id=1, source_target_pairs={{0,1},{1,2},{2,3},{3,0},{4,5},{5,6},{6,7},{7,4},{8,9},{9,10},{10,1... | collective-permute-start | bytes 786440 | tf_op jit(solution)/shard_map/ppermute | solution.py:63
  (29 other events, 222.5 us)
